TPU v7x, 32 devices: a whole 2x2x4 slice. The times are simulated.
32 devices in a mesh: rep: 4 (over x, y), dp: 8 (over z, core).
Axes of the slice: x: 2, y: 2, z: 4, core: 2. Of those that a mesh axis runs over, the one named last changes fastest.
Arguments:
- g_w_gate: bfloat16 [32, 2, 1280, 4480], P(('rep', 'dp')), parts along dimension 0
- g_w_up: bfloat16 [32, 2, 1280, 4480], P(('rep', 'dp')), parts along dimension 0
- g_w_down: bfloat16 [32, 2, 4480, 1280], P(('rep', 'dp')), parts along dimension 0
- w_gate: bfloat16 [2, 1280, 4480], replicated
- w_up: bfloat16 [2, 1280, 4480], replicated
- w_down: bfloat16 [2, 4480, 1280], replicated
- m_w_gate: float32 [2, 1280, 4480], P(None, 'dp')
- m_w_up: float32 [2, 1280, 4480], P(None, 'dp')
- m_w_down: float32 [2, 4480, 1280], P(None, 'dp')
- v_w_gate: float32 [2, 1280, 4480], P(None, 'dp')
- v_w_up: float32 [2, 1280, 4480], P(None, 'dp')
- v_w_down: float32 [2, 4480, 1280], P(None, 'dp')
Outputs:
- output 1: bfloat16 [8, 1280, 4480], P('rep'), parts along dimension 0
- output 2: bfloat16 [8, 1280, 4480], P('rep'), parts along dimension 0
- output 3: bfloat16 [8, 4480, 1280], P('rep'), parts along dimension 0
- output 4: float32 [8, 1280, 4480], P('rep', 'dp'), parts along dimension 0
- output 5: float32 [8, 1280, 4480], P('rep', 'dp'), parts along dimension 0
- output 6: float32 [8, 4480, 1280], P('rep', 'dp'), parts along dimension 0
- output 7: float32 [8, 1280, 4480], P('rep', 'dp'), parts along dimension 0
- output 8: float32 [8, 1280, 4480], P('rep', 'dp'), parts along dimension 0
- output 9: float32 [8, 4480, 1280], P('rep', 'dp'), parts along dimension 0
There are 4 independent parts. A program takes and returns all parts, laid end to end along the dimension named above; an argument that names none is the same for every part.
All inputs are finite; a program needn't handle non-finite values.
Results may differ from a plain program's by a relative error of at most 0.022.
Values are sent between devices in bfloat16 or wider.
A program may use at most 2 GiB of HBM per device.

v0:
```python
import jax
import jax.numpy as jnp
from jax import lax
from jax.sharding import PartitionSpec as P


def adamw(w, m, v, g):
    m = 0.9 * m + 0.1 * g
    v = 0.95 * v + 0.05 * g * g
    step = m * lax.rsqrt(v + 1e-8) + 0.1 * w
    return (w - 0.02 * step).astype(jnp.bfloat16), m, v


def solution(mesh):
    def step(*arrays):
        terms, weights, m, v = (arrays[i : i + 3] for i in (0, 3, 6, 9))
        gradients = [lax.psum_scatter(t[0], "dp", scatter_dimension=1, tiled=True).astype(jnp.float32) for t in terms]
        me = lax.axis_index("dp")
        own = [lax.dynamic_slice_in_dim(w, me * one.shape[1], one.shape[1], 1).astype(jnp.float32) for w, one in zip(weights, m, strict=True)]
        new = [adamw(w, m, v, g) for w, m, v, g in zip(own, m, v, gradients, strict=True)]
        whole = [lax.all_gather(one[0], "dp", axis=1, tiled=True) for one in new]
        return (*whole, *(one[1] for one in new), *(one[2] for one in new))

    all_of, cut = P(None, None, None), P(None, "dp", None)
    return jax.shard_map(
        step,
        mesh=mesh,
        in_specs=(P(("rep", "dp"), None, None, None),) * 3 + (all_of,) * 3 + (cut,) * 6,
        out_specs=(P("rep", None, None),) * 3 + (P("rep", "dp", None),) * 6,
        check_vma=False,
    )
```

profile of v0, /device:TPU:0, one launch (start us, length us, event | category | flops | bytes accessed | tf_op | source)
XLA Modules:
  0.0 1354.2 jit_solution(14291681878599793402)
XLA Ops:
  7.2 0.0 reduce-scatter.8.cloned.1.call-start
  7.2 0.7 reduce-scatter.8.cloned.1.call-update
  7.9 0.0 reduce-scatter.6.cloned.1.call-start
  8.0 0.7 reduce-scatter.6.cloned.1.call-update
  8.7 0.0 reduce-scatter.4.cloned.1.call-start
  8.7 0.7 reduce-scatter.4.cloned.1.call-update
  9.4 0.0 all-gather.8.cloned.1.call-start
  9.4 229.6 %reduce-scatter.8.cloned.1.call-done = bf16[2,560,1280]{2,1,0:T(8,128)(2,1)} async-done(((bf16[2,4480,1280]{2,1,0:T(8,128)(2,1)}), bf16[2,560,1280]{2,1,0:T(8,128)(2,1)}) %reduce-scatter.8.cloned.1.call-update) | async-done | bytes 2867216 | tf_op jit(solution)/shard_map/reduce_scatter | solution.py:17
  239.1 11.9 fusion.10
  251.0 0.0 all-gather.8.cloned.1.call-update
  251.0 0.0 all-gather.6.cloned.1.call-start
  251.0 215.1 %reduce-scatter.6.cloned.1.call-done = bf16[2,160,4480]{2,1,0:T(8,128)(2,1)} async-done(((bf16[2,1280,4480]{2,1,0:T(8,128)(2,1)}), bf16[2,160,4480]{2,1,0:T(8,128)(2,1)}) %reduce-scatter.6.cloned.1.call-update) | async-done | bytes 2867216 | tf_op jit(solution)/shard_map/reduce_scatter | solution.py:17
  466.2 11.9 fusion.6
  478.0 0.0 all-gather.6.cloned.1.call-update
  478.1 0.0 all-gather.4.cloned.1.call-start
  478.1 215.1 %reduce-scatter.4.cloned.1.call-done = bf16[2,160,4480]{2,1,0:T(8,128)(2,1)} async-done(((bf16[2,1280,4480]{2,1,0:T(8,128)(2,1)}), bf16[2,160,4480]{2,1,0:T(8,128)(2,1)}) %reduce-scatter.4.cloned.1.call-update) | async-done | bytes 2867216 | tf_op jit(solution)/shard_map/reduce_scatter | solution.py:17
  693.3 11.9 fusion.2
  705.1 0.0 all-gather.4.cloned.1.call-update
  705.1 190.8 %all-gather.8.cloned.1.call-done = bf16[2,4480,1280]{2,1,0:T(8,128)(2,1)} async-done(((bf16[2,560,1280]{2,1,0:T(8,128)(2,1)}), bf16[2,4480,1280]{2,1,0:T(8,128)(2,1)}) %all-gather.8.cloned.1.call-update) | async-done | bytes 22937616 | tf_op jit(solution)/shard_map/all_gather | solution.py:21
  896.0 202.7 %all-gather.6.cloned.1.call-done = bf16[2,1280,4480]{2,1,0:T(8,128)(2,1)} async-done(((bf16[2,160,4480]{2,1,0:T(8,128)(2,1)}), bf16[2,1280,4480]{2,1,0:T(8,128)(2,1)}) %all-gather.6.cloned.1.call-update) | async-done | bytes 22937616 | tf_op jit(solution)/shard_map/all_gather | solution.py:21
  1098.7 202.7 %all-gather.4.cloned.1.call-done = bf16[2,1280,4480]{2,1,0:T(8,128)(2,1)} async-done(((bf16[2,160,4480]{2,1,0:T(8,128)(2,1)}), bf16[2,1280,4480]{2,1,0:T(8,128)(2,1)}) %all-gather.4.cloned.1.call-update) | async-done | bytes 22937616 | tf_op jit(solution)/shard_map/all_gather | solution.py:21
  1301.5 19.0 %copy.24 = bf16[2,1280,4480]{2,1,0:T(8,128)(2,1)} copy(bf16[2,1280,4480]{2,1,0:T(8,128)(2,1)} %all-gather.4.cloned.1.call-done) | data formatting | bytes 45875200
  1320.4 18.7 %copy.25 = bf16[2,1280,4480]{2,1,0:T(8,128)(2,1)} copy(bf16[2,1280,4480]{2,1,0:T(8,128)(2,1)} %all-gather.6.cloned.1.call-done) | data formatting | bytes 45875200
  1339.2 8.2 copy.26
  (13 shorter events, 0.0 us)
Async XLA Ops:
  7.2 231.9 %reduce-scatter.8.cloned.1.call-start = ((), (), s32[]{:S(2)}) async-start(), calls=%async_computation.7 | async-start | bytes 25804800 | tf_op jit(solution)/shard_map/reduce_scatter | solution.py:17
  7.9 458.3 %reduce-scatter.6.cloned.1.call-start = ((), (), s32[]{:S(2)}) async-start(), calls=%async_computation.5 | async-start | bytes 25804800 | tf_op jit(solution)/shard_map/reduce_scatter | solution.py:17
  8.7 684.6 %reduce-scatter.4.cloned.1.call-start = ((), (), s32[]{:S(2)}) async-start(), calls=%async_computation.3 | async-start | bytes 25804800 | tf_op jit(solution)/shard_map/reduce_scatter | solution.py:17
  9.4 886.6 %all-gather.8.cloned.1.call-start = ((), (), s32[]{:S(2)}) async-start(), calls=%async_computation.8 | async-start | bytes 25804800 | tf_op jit(solution)/shard_map/all_gather | solution.py:21
  251.0 847.7 %all-gather.6.cloned.1.call-start = ((), (), s32[]{:S(2)}) async-start(), calls=%async_computation.6 | async-start | bytes 25804800 | tf_op jit(solution)/shard_map/all_gather | solution.py:21
  478.1 823.4 %all-gather.4.cloned.1.call-start = ((), (), s32[]{:S(2)}) async-start(), calls=%async_computation.4 | async-start | bytes 25804800 | tf_op jit(solution)/shard_map/all_gather | solution.py:21
  1301.5 37.7 %slice-start = ((s8[22937600]{0:T(1024)(128)(4,1)}), s8[4194304]{0:T(1024)(128)(4,1)S(1)}, s32[]{:S(2)}) async-start(s8[22937600]{0:T(1024)(128)(4,1)} %bitcast.6), calls=%async_computation.9 | async-start | bytes 8388608
  1301.5 37.7 %slice-start.1 = ((s8[22937600]{0:T(1024)(128)(4,1)}), s8[4194304]{0:T(1024)(128)(4,1)S(1)}, s32[]{:S(2)}) async-start(s8[22937600]{0:T(1024)(128)(4,1)} %bitcast.6), calls=%async_computation.10 | async-start | bytes 8388608
  1301.5 37.7 %slice-start.2 = ((s8[22937600]{0:T(1024)(128)(4,1)}), s8[4194304]{0:T(1024)(128)(4,1)S(1)}, s32[]{:S(2)}) async-start(s8[22937600]{0:T(1024)(128)(4,1)} %bitcast.6), calls=%async_computation.11 | async-start | bytes 8388608
  1320.4 18.7 %slice-start.3 = ((s8[22937600]{0:T(1024)(128)(4,1)}), s8[4194304]{0:T(1024)(128)(4,1)S(1)}, s32[]{:S(2)}) async-start(s8[22937600]{0:T(1024)(128)(4,1)} %bitcast.6), calls=%async_computation.12 | async-start | bytes 8388608
  1320.4 18.7 %slice-start.4 = ((s8[22937600]{0:T(1024)(128)(4,1)}), s8[4194304]{0:T(1024)(128)(4,1)S(1)}, s32[]{:S(2)}) async-start(s8[22937600]{0:T(1024)(128)(4,1)} %bitcast.6), calls=%async_computation.13 | async-start | bytes 8388608
  1320.4 18.7 %slice-start.5 = ((s8[22937600]{0:T(1024)(128)(4,1)}), s8[1966080]{0:T(1024)(128)(4,1)S(1)}, s32[]{:S(2)}) async-start(s8[22937600]{0:T(1024)(128)(4,1)} %bitcast.6), calls=%async_computation.14 | async-start | bytes 3932160
Sparse Core Ops, SparseCore 0:
  10.4 228.6 reduce-scatter.7
  241.5 224.6 reduce-scatter.5
  468.6 224.6 reduce-scatter.3
  695.3 200.6 all-gather.7
  898.0 200.6 all-gather.5
  1100.7 200.6 all-gather.3
where the time goes:
time: 1350 us
  waiting for transfers between devices  1260 us (93%)
  local copies, waits for them, and re-layouts  45.9 us (3%)
  other arithmetic  35.6 us (3%)
  between operations  14.2 us (1%)
    reduce_scatter x3, waiting for transfers between devices, step(): lax.psum_scatter(t[0], 'dp', scatter_dimension=1, tiled=True)  660 us
    all_gather x3, waiting for transfers between devices, step(): whole = [lax.all_gather(one[0], 'dp', axis=1, tiled=True) for one in new]  596 us
    unnamed x15, local copies, waits for them, and re-layouts  45.9 us
    convert_element_type x3, other arithmetic, adamw(): return ((w - 0.02 * step).astype(jnp.bfloat16), m, v)  35.6 us
  transfers between devices with their start and end apart: 6, of which 6 were waited for; matrix products, arithmetic and copies ran while one was open for 3% of the time, Pallas kernels for 0%

commit v1 on v0

v1 whole, which is shorter than its diff:
```python
import functools

import jax
import jax.numpy as jnp
from jax import lax
from jax.experimental import pallas as pl
from jax.experimental.pallas import tpu as pltpu
from jax.sharding import PartitionSpec as P

MESH = pl.DeviceIdType.MESH
CHIPS = 4
TILES = 35
HOP = 1
HOP2 = 1
LAG = 3
S_RAW, S_IN, S_OUT, S_ADAM, S_AG = 12, 8, 4, 3, 16
PIECE = 40


def tiles(x):
    *lead, r, c = x.shape
    return x.reshape(*lead, r // 8, 8, c // 128, 128).swapaxes(-3, -2).reshape(*lead, r * c // 128, 128)


def untiles(x, r, c):
    lead = x.shape[:-2]
    return x.reshape(*lead, r // 8, c // 128, 8, 128).swapaxes(-3, -2).reshape(*lead, r, c)


def kernel(
    per_layer, layers, *refs
):
    g, w, m, v = (refs[i : i + 3] for i in (0, 3, 6, 9))
    new_w, new_m, new_v = refs[12:15]
    own, sib, rin, lin, rout, lout, total, mi, vi, wi, mo, vo, wo = refs[15:28]
    own_sem, raw_s, raw_r, rs, rr, ls, lr, ld_sem, st_sem, own_s, fwd_s, ag_r, sib_s, sib_r = refs[28:]
    rows_per = TILES * 8
    n = len(g) * layers * per_layer
    d = lax.axis_index("dp")
    z, c = lax.div(d, 2), lax.rem(d, 2)
    right, left, twin = {"dp": lax.rem(d + 2, 8)}, {"dp": lax.rem(d + 6, 8)}, {"dp": z * 2 + 1 - c}
    far = jnp.maximum(z, CHIPS - 1 - z)

    def turn(o):
        return LAG + HOP * jnp.maximum(o, CHIPS - 1 - o)

    def place(i):
        which, rest = lax.div(i, layers * per_layer), lax.rem(i, layers * per_layer)
        layer, k = lax.div(rest, per_layer), lax.rem(rest, per_layer)
        return which, layer, pl.ds(pl.multiple_of(k * rows_per, 8), rows_per)

    def inside(i):
        return (i >= 0) & (i < n)

    def remote(src, dst, s, r, to):
        return pltpu.make_async_remote_copy(src, dst, s, r, device_id=to, device_id_type=MESH)

    def pieces(body):
        def one(p, _):
            body(pl.ds(pl.multiple_of(p * PIECE, 8), PIECE))
            return 0

        lax.fori_loop(0, rows_per // PIECE, one, 0)

    def f32(ref):
        return ref[...].astype(jnp.float32)

    barrier = pltpu.get_barrier_semaphore()

    @pl.when(z < CHIPS - 1)
    def _():
        pl.semaphore_signal(barrier, 1, device_id=right, device_id_type=MESH)

    @pl.when(z > 0)
    def _():
        pl.semaphore_signal(barrier, 1, device_id=left, device_id_type=MESH)

    pl.semaphore_signal(barrier, 1, device_id=twin, device_id_type=MESH)
    pl.semaphore_wait(barrier, 1 + (z > 0).astype(jnp.int32) + (z < CHIPS - 1).astype(jnp.int32))

    def raw(i):
        which, layer, rows = place(i)
        s = lax.rem(i, S_RAW)
        return which, [
            (
                pltpu.make_async_copy(one.at[layer, :, c, rows], own.at[s], own_sem.at[s]),
                remote(one.at[layer, :, 1 - c, rows], sib.at[s], raw_s.at[s], raw_r.at[s], twin),
            )
            for one in g
        ]

    def fetch(t):
        i = t

        @pl.when(inside(i))
        def _():
            which, copies = raw(i)

            @pl.when(i >= S_RAW)
            def _():
                copies[0][1].wait_send()

            for one, (mine, other) in enumerate(copies):

                @pl.when(which == one)
                def _():
                    other.start()
                    mine.start()

    def arrived(i):
        _, copies = raw(i)
        copies[0][0].wait()
        copies[0][1].wait_recv()

    def passing(t, rightward):
        if rightward:
            before, box, out, s_sem, r_sem, to = z, rin, rout, rs, rr, right
            many, has_in = CHIPS - 1 - z, z > 0
            first = z <= 1
            lane_of = lambda k: CHIPS - 1 - k
        else:
            before, box, out, s_sem, r_sem, to = CHIPS - 1 - z, lin, lout, ls, lr, left
            many, has_in = z, z < CHIPS - 1
            first = z > 1
            lane_of = lambda k: k
        i = t - LAG - HOP * before

        @pl.when(inside(i))
        def _():
            raw_slot, in_slot, out_slot = lax.rem(i, S_RAW), lax.rem(i, S_IN), lax.rem(i, S_OUT)

            def copy(o):
                return remote(out.at[out_slot, o], box.at[in_slot, o], s_sem.at[out_slot, o], r_sem.at[in_slot, o], to)

            @pl.when(first)
            def _():
                arrived(i)

            def lane(k, _):
                o = lane_of(k)

                @pl.when(i >= S_OUT)
                def _():
                    copy(o).wait_send()

                @pl.when(has_in)
                def _():
                    copy(o).wait_recv()

                    def add(rows):
                        so_far = f32(own.at[raw_slot, o, rows]) + f32(sib.at[raw_slot, o, rows])
                        out[out_slot, o, rows] = (so_far + f32(box.at[in_slot, o, rows])).astype(jnp.bfloat16)

                    pieces(add)

                @pl.when(jnp.logical_not(has_in))
                def _():
                    def add(rows):
                        so_far = f32(own.at[raw_slot, o, rows]) + f32(sib.at[raw_slot, o, rows])
                        out[out_slot, o, rows] = so_far.astype(jnp.bfloat16)

                    pieces(add)

                copy(o).start()
                return 0

            lax.fori_loop(0, many, lane, 0)

            @pl.when(has_in)
            def _():
                copy(z).wait_recv()

    def loads(i):
        which, layer, rows = place(i)
        s = lax.rem(i, S_ADAM)
        return which, [
            (
                pltpu.make_async_copy(m[one].at[layer, rows], mi.at[s], ld_sem.at[s, 0]),
                pltpu.make_async_copy(v[one].at[layer, rows], vi.at[s], ld_sem.at[s, 1]),
                pltpu.make_async_copy(w[one].at[layer, d, rows], wi.at[s], ld_sem.at[s, 2]),
            )
            for one in range(3)
        ]

    def fetch_state(t):
        i = t - turn(z) + S_ADAM - 1

        @pl.when(inside(i))
        def _():
            which, copies = loads(i)
            for one, each in enumerate(copies):

                @pl.when(which == one)
                def _():
                    for copy in each:
                        copy.start()

    def stores(i):
        which, layer, rows = place(i)
        s, a = lax.rem(i, S_ADAM), lax.rem(i, S_AG)
        there = new_w.at[which, layer, d, rows]
        local = [
            pltpu.make_async_copy(mo.at[s], new_m.at[which, layer, rows], st_sem.at[s, 0]),
            pltpu.make_async_copy(vo.at[s], new_v.at[which, layer, rows], st_sem.at[s, 1]),
            pltpu.make_async_copy(wo.at[s], there, st_sem.at[s, 2]),
        ]
        to_right = remote(wo.at[s], there, own_s.at[s, 0], ag_r.at[a, z], right)
        to_left = remote(wo.at[s], there, own_s.at[s, 1], ag_r.at[a, z], left)
        to_twin = remote(wo.at[s], there, own_s.at[s, 2], sib_r.at[a, z], twin)
        return local, to_right, to_left, to_twin

    def stored(i):
        local, to_right, to_left, to_twin = stores(i)
        for copy in local:
            copy.wait()
        to_twin.wait_send()

        @pl.when(z < CHIPS - 1)
        def _():
            to_right.wait_send()

        @pl.when(z > 0)
        def _():
            to_left.wait_send()

    def adam(t):
        i = t - turn(z)

        @pl.when(inside(i))
        def _():
            raw_slot, in_slot, s = lax.rem(i, S_RAW), lax.rem(i, S_IN), lax.rem(i, S_ADAM)
            _, copies = loads(i)
            for copy in copies[0]:
                copy.wait()

            @pl.when(i >= S_ADAM)
            def _():
                stored(i - S_ADAM)

            def begin(rows):
                total[rows] = f32(own.at[raw_slot, z, rows]) + f32(sib.at[raw_slot, z, rows])

            pieces(begin)

            @pl.when(z > 0)
            def _():
                def add(rows):
                    total[rows] += f32(rin.at[in_slot, z, rows])

                pieces(add)

            @pl.when(z < CHIPS - 1)
            def _():
                def add(rows):
                    total[rows] += f32(lin.at[in_slot, z, rows])

                pieces(add)

            def step(rows):
                grad = total[rows].astype(jnp.bfloat16).astype(jnp.float32)
                m1 = 0.9 * mi[s, rows] + 0.1 * grad
                v1 = 0.95 * vi[s, rows] + 0.05 * grad * grad
                w0 = f32(wi.at[s, rows])
                mo[s, rows] = m1
                vo[s, rows] = v1
                wo[s, rows] = (w0 - 0.02 * (m1 * lax.rsqrt(v1 + 1e-8) + 0.1 * w0)).astype(jnp.bfloat16)

            pieces(step)
            local, to_right, to_left, to_twin = stores(i)

            @pl.when(z < CHIPS - 1)
            def _():
                to_right.start()

            @pl.when(z > 0)
            def _():
                to_left.start()

            to_twin.start()
            for copy in local:
                copy.start()

    def forwards(i, o, to):
        which, layer, rows = place(i)
        a = lax.rem(i, S_AG)
        there = new_w.at[which, layer, o * 2 + c, rows]
        return remote(there, there, fwd_s.at[a, o], ag_r.at[a, o], to), remote(there, there, sib_s.at[a, o], sib_r.at[a, o], twin)

    def sent(i, o, to, on):
        ahead, across = forwards(i, o, to)

        @pl.when(on)
        def _():
            ahead.wait_send()

        across.wait_send()

    def gathering(t, rightward):
        many, to, on = (z, right, z < CHIPS - 1) if rightward else (CHIPS - 1 - z, left, z > 0)

        def lane(k, _):
            o = z - 1 - k if rightward else z + 1 + k
            i = t - turn(o) - HOP2 * (k + 1)

            @pl.when(inside(i))
            def _():
                @pl.when(i >= S_AG)
                def _():
                    sent(i - S_AG, o, to, on)

                ahead, across = forwards(i, o, to)
                ahead.wait_recv()

                @pl.when(on)
                def _():
                    ahead.start()

                across.start()

            return 0

        lax.fori_loop(0, many, lane, 0)

    def crossing(t):
        def lane(o, _):
            i = t - turn(o) - HOP2 * jnp.abs(z - o) - 2

            @pl.when(inside(i))
            def _():
                forwards(i, o, right)[1].wait_recv()

            return 0

        lax.fori_loop(0, CHIPS, lane, 0)

    def step(t, _):
        passing(t, True)
        passing(t, False)
        adam(t)
        gathering(t, True)
        gathering(t, False)
        fetch(t)
        fetch_state(t)
        crossing(t)
        return 0

    lax.fori_loop(0, n + LAG + (HOP + HOP2) * (CHIPS - 1) + 3, step, 0)

    def raw_left(k, _):
        raw(n - S_RAW + k)[1][0][1].wait_send()
        return 0

    lax.fori_loop(0, S_RAW, raw_left, 0)

    def pass_left(k, _):
        i = n - S_OUT + k
        s, e = lax.rem(i, S_OUT), lax.rem(i, S_IN)

        def to_right(o, _):
            remote(rout.at[s, o], rin.at[e, o], rs.at[s, o], rr.at[e, o], right).wait_send()
            return 0

        def to_left(o, _):
            remote(lout.at[s, o], lin.at[e, o], ls.at[s, o], lr.at[e, o], left).wait_send()
            return 0

        lax.fori_loop(z + 1, CHIPS, to_right, 0)
        lax.fori_loop(0, z, to_left, 0)
        return 0

    lax.fori_loop(0, S_OUT, pass_left, 0)

    def stores_left(k, _):
        stored(n - S_ADAM + k)
        return 0

    lax.fori_loop(0, S_ADAM, stores_left, 0)

    def gather_left(k, _):
        i = n - S_AG + k

        def of_left(o, _):
            sent(i, o, right, z < CHIPS - 1)
            return 0

        def of_right(o, _):
            sent(i, o, left, z > 0)
            return 0

        lax.fori_loop(0, z, of_left, 0)
        lax.fori_loop(z + 1, CHIPS, of_right, 0)
        return 0

    lax.fori_loop(0, S_AG, gather_left, 0)


def solution(mesh):
    bf16, f32 = jnp.bfloat16, jnp.float32

    def step(*arrays):
        terms, weights, m, v = (arrays[i : i + 3] for i in (0, 3, 6, 9))
        layers = weights[0].shape[0]
        block = weights[0].shape[1] * weights[0].shape[2] // (2 * CHIPS * 128)
        rows = TILES * 8
        args = [tiles(t[0]).reshape(layers, CHIPS, 2, block, 128) for t in terms]
        args += [tiles(w).reshape(layers, 2 * CHIPS, block, 128) for w in weights]
        args += [tiles(x) for x in (*m, *v)]
        dma = pltpu.SemaphoreType.DMA
        new_w, new_m, new_v = pl.pallas_call(
            functools.partial(kernel, block // rows, layers),
            out_shape=[
                jax.ShapeDtypeStruct((3, layers, 2 * CHIPS, block, 128), bf16),
                jax.ShapeDtypeStruct((3, layers, block, 128), f32),
                jax.ShapeDtypeStruct((3, layers, block, 128), f32),
            ],
            in_specs=[pl.BlockSpec(memory_space=pl.ANY)] * 12,
            out_specs=[pl.BlockSpec(memory_space=pl.ANY)] * 3,
            scratch_shapes=[
                pltpu.VMEM((S_RAW, CHIPS, rows, 128), bf16),
                pltpu.VMEM((S_RAW, CHIPS, rows, 128), bf16),
                pltpu.VMEM((S_IN, CHIPS, rows, 128), bf16),
                pltpu.VMEM((S_IN, CHIPS, rows, 128), bf16),
                pltpu.VMEM((S_OUT, CHIPS, rows, 128), bf16),
                pltpu.VMEM((S_OUT, CHIPS, rows, 128), bf16),
                pltpu.VMEM((rows, 128), f32),
                pltpu.VMEM((S_ADAM, rows, 128), f32),
                pltpu.VMEM((S_ADAM, rows, 128), f32),
                pltpu.VMEM((S_ADAM, rows, 128), bf16),
                pltpu.VMEM((S_ADAM, rows, 128), f32),
                pltpu.VMEM((S_ADAM, rows, 128), f32),
                pltpu.VMEM((S_ADAM, rows, 128), bf16),
                dma((S_RAW,)),
                dma((S_RAW,)),
                dma((S_RAW,)),
                dma((S_OUT, CHIPS)),
                dma((S_IN, CHIPS)),
                dma((S_OUT, CHIPS)),
                dma((S_IN, CHIPS)),
                dma((S_ADAM, 3)),
                dma((S_ADAM, 3)),
                dma((S_ADAM, 3)),
                dma((S_AG, CHIPS)),
                dma((S_AG, CHIPS)),
                dma((S_AG, CHIPS)),
                dma((S_AG, CHIPS)),
            ],
            compiler_params=pltpu.CompilerParams(collective_id=0, has_side_effects=True),
        )(*args)
        outs = [untiles(new_w[k].reshape(layers, -1, 128), *weights[k].shape[1:]) for k in range(3)]
        for new, old in ((new_m, m), (new_v, v)):
            outs += [untiles(new[k], *old[k].shape[1:]) for k in range(3)]
        return tuple(outs)

    all_of, cut = P(None, None, None), P(None, "dp", None)
    return jax.shard_map(
        step,
        mesh=mesh,
        in_specs=(P(("rep", "dp"), None, None, None),) * 3 + (all_of,) * 3 + (cut,) * 6,
        out_specs=(P("rep", None, None),) * 3 + (P("rep", "dp", None),) * 6,
        check_vma=False,
    )
```

time: 1350 us -> 835 us (0.62)
  waiting for transfers between devices: 1260 us -> 0 us
  Pallas kernels: 0 us -> 763 us
  other arithmetic: 35.6 us -> 0 us
  local copies, waits for them, and re-layouts: 45.9 us -> 70.2 us
  between operations: 14.2 us -> 0.66 us
    pallas_call x0 -> x1, Pallas kernels: none -> 763 us  [step(): pl.pallas_call(functools.partial(kernel, block // rows, layers), out_shap...]
    reduce_scatter x3 -> x0, waiting for transfers between devices: 660 us -> none  [step(): lax.psum_scatter(t[0], 'dp', scatter_dimension=1, tiled=True)]
    all_gather x3 -> x0, waiting for transfers between devices: 596 us -> none  [step(): whole = [lax.all_gather(one[0], 'dp', axis=1, tiled=True) for one in new]]
    slice x0 -> x2, local copies, waits for them, and re-layouts: none -> 70.2 us  [the longest x1 46.1 us: step(): new_w[k].reshape(layers, -1, 128)]
    unnamed x15 -> x0, local copies, waits for them, and re-layouts: 45.9 us -> none
    convert_element_type x3 -> x0, other arithmetic: 35.6 us -> none  [adamw(): return ((w - 0.02 * step).astype(jnp.bfloat16), m, v)]
  transfers between devices with their start and end apart: 6 -> 0, of which waited for: 6 -> 0; matrix products, arithmetic and copies ran while one was open for 3% -> 0% of each run, Pallas kernels for 0% -> 0%
where the time goes in v1:
time: 835 us; the launch traced here: 834 us
  Pallas kernels  763 us (91%)
  local copies, waits for them, and re-layouts  70.2 us (8%)
    pallas_call x1, Pallas kernels, step(): pl.pallas_call(functools.partial(kernel, block // rows, layers), out_shap...  763 us
    slice x1, local copies, waits for them, and re-layouts, step(): new_w[k].reshape(layers, -1, 128)  46.1 us
    slice x1, local copies, waits for them, and re-layouts, step(): outs += [untiles(new[k], *old[k].shape[1:]) for k in range(3)]  24.1 us

profile of v1, /device:TPU:0, one launch (start us, length us, event | category | flops | bytes accessed | tf_op | source)
XLA Modules:
  0.0 834.0 jit_solution(5792869417272009749)
XLA Ops:
  0.6 763.2 %shard_map.187 = (bf16[3,2,8,5600,128]{4,3,2,1,0:T(8,128)(2,1)}, f32[3,2,5600,128]{3,2,1,0:T(8,128)}, f32[3,2,5600,128]{3,2,1,0:T(8,128)}) custom-call(bf16[2,4,2,5600,128]{4,3,2,1,0:T(8,128)(2,1)} %bitcast.105, bf16[2,4,2,5600,128]{4,3,2,1,0:T(8,128)(2,1)} %bitcast.106, bf16[2,4,2,5600,128]{4,3,2,1,0:T(8,128)(2,1)} %bitcast.107, ...), custom_call_target="tpu_custom_call" | custom-call | tf_op jit(solution)/shard_map/pallas_call | solution.py:409
  763.9 46.1 %fusion = (bf16[1,2,8,5600,128]{4,3,2,1,0:T(8,128)(2,1)}, bf16[1,2,8,5600,128]{4,3,2,1,0:T(8,128)(2,1)}, bf16[1,2,8,5600,128]{4,3,2,1,0:T(8,128)(2,1)}) fusion(bf16[3,2,8,5600,128]{4,3,2,1,0:T(8,128)(2,1)} %get-tuple-element.12), kind=kLoop, calls=%fused_computation | loop fusion | bytes 137625600 | tf_op jit(solution)/shard_map/slice | solution.py:449
  810.0 24.1 %fusion.1 = (f32[1,2,5600,128]{3,2,1,0:T(8,128)}, f32[1,2,5600,128]{3,2,1,0:T(8,128)}, f32[1,2,5600,128]{3,2,1,0:T(8,128)}, f32[1,2,5600,128]{3,2,1,0:T(8,128)},...) fusion(f32[3,2,5600,128]{3,2,1,0:T(8,128)} %get-tuple-element.14, f32[3,2,5600,128]{3,2,1,0:T(8,128)} %get-tuple-element.13), kind=kLoop, calls=%fused_computation.1 | loop fusion | bytes 68812800 | tf_op jit(solution)/shard_map/slice | solution.py:451

commit v2 on v1

--- a/solution.py
+++ b/solution.py
@@ -9,12 +9,14 @@
 
 MESH = pl.DeviceIdType.MESH
 CHIPS = 4
-TILES = 35
+TILES = 28
 HOP = 1
 HOP2 = 1
-LAG = 3
-S_RAW, S_IN, S_OUT, S_ADAM, S_AG = 12, 8, 4, 3, 16
-PIECE = 40
+LAG = 2
+S_RAW, S_IN, S_OUT, S_ADAM, S_AG = 10, 6, 3, 3, 16
+ROOM = 9472 * 1024
+SPANS, S_COPY = 32, 12
+PIECE = 32
 
 
 def tiles(x):
@@ -31,9 +33,10 @@
     per_layer, layers, *refs
 ):
     g, w, m, v = (refs[i : i + 3] for i in (0, 3, 6, 9))
-    new_w, new_m, new_v = refs[12:15]
-    own, sib, rin, lin, rout, lout, total, mi, vi, wi, mo, vo, wo = refs[15:28]
-    own_sem, raw_s, raw_r, rs, rr, ls, lr, ld_sem, st_sem, own_s, fwd_s, ag_r, sib_s, sib_r = refs[28:]
+    new_w, last_w, state = refs[12:15]
+    new_m, new_v = state.at[0], state.at[1]
+    own, sib, rin, lin, rout, lout, total, wi, wo = refs[15:24]
+    own_sem, raw_s, raw_r, rs, rr, ls, lr, ld_sem, st_sem, own_s, fwd_s, ag_r, sib_s, sib_r = refs[24:]
     rows_per = TILES * 8
     n = len(g) * layers * per_layer
     d = lax.axis_index("dp")
@@ -48,6 +51,11 @@
         which, rest = lax.div(i, layers * per_layer), lax.rem(i, layers * per_layer)
         layer, k = lax.div(rest, per_layer), lax.rem(rest, per_layer)
         return which, layer, pl.ds(pl.multiple_of(k * rows_per, 8), rows_per)
+
+    def spots(i, owner):
+        which, layer, rows = place(i)
+        late = i >= n - per_layer
+        return (jnp.logical_not(late), new_w.at[which, layer, owner, rows]), (late, last_w.at[owner, rows])
 
     def inside(i):
         return (i >= 0) & (i < n)
@@ -175,8 +183,8 @@
         s = lax.rem(i, S_ADAM)
         return which, [
             (
-                pltpu.make_async_copy(m[one].at[layer, rows], mi.at[s], ld_sem.at[s, 0]),
-                pltpu.make_async_copy(v[one].at[layer, rows], vi.at[s], ld_sem.at[s, 1]),
+                pltpu.make_async_copy(m[one].at[layer, rows], new_m.at[one, layer, rows], ld_sem.at[s, 0]),
+                pltpu.make_async_copy(v[one].at[layer, rows], new_v.at[one, layer, rows], ld_sem.at[s, 1]),
                 pltpu.make_async_copy(w[one].at[layer, d, rows], wi.at[s], ld_sem.at[s, 2]),
             )
             for one in range(3)
@@ -195,24 +203,22 @@
                     for copy in each:
                         copy.start()
 
-    def stores(i):
-        which, layer, rows = place(i)
+    def stores(i, there):
         s, a = lax.rem(i, S_ADAM), lax.rem(i, S_AG)
-        there = new_w.at[which, layer, d, rows]
-        local = [
-            pltpu.make_async_copy(mo.at[s], new_m.at[which, layer, rows], st_sem.at[s, 0]),
-            pltpu.make_async_copy(vo.at[s], new_v.at[which, layer, rows], st_sem.at[s, 1]),
-            pltpu.make_async_copy(wo.at[s], there, st_sem.at[s, 2]),
-        ]
+        local = pltpu.make_async_copy(wo.at[s], there, st_sem.at[s])
         to_right = remote(wo.at[s], there, own_s.at[s, 0], ag_r.at[a, z], right)
         to_left = remote(wo.at[s], there, own_s.at[s, 1], ag_r.at[a, z], left)
         to_twin = remote(wo.at[s], there, own_s.at[s, 2], sib_r.at[a, z], twin)
         return local, to_right, to_left, to_twin
 
     def stored(i):
-        local, to_right, to_left, to_twin = stores(i)
-        for copy in local:
-            copy.wait()
+        (in_hbm, there), _ = spots(i, d)
+        local, to_right, to_left, to_twin = stores(i, there)
+
+        @pl.when(in_hbm)
+        def _():
+            local.wait()
+
         to_twin.wait_send()
 
         @pl.when(z < CHIPS - 1)
@@ -256,38 +262,51 @@
 
                 pieces(add)
 
+            which, layer, base = place(i)
+
             def step(rows):
+                to = pl.ds(pl.multiple_of(base.start + rows.start, 8), PIECE)
                 grad = total[rows].astype(jnp.bfloat16).astype(jnp.float32)
-                m1 = 0.9 * mi[s, rows] + 0.1 * grad
-                v1 = 0.95 * vi[s, rows] + 0.05 * grad * grad
+                m1 = 0.9 * new_m[which, layer, to] + 0.1 * grad
+                v1 = 0.95 * new_v[which, layer, to] + 0.05 * grad * grad
                 w0 = f32(wi.at[s, rows])
-                mo[s, rows] = m1
-                vo[s, rows] = v1
+                new_m[which, layer, to] = m1
+                new_v[which, layer, to] = v1
                 wo[s, rows] = (w0 - 0.02 * (m1 * lax.rsqrt(v1 + 1e-8) + 0.1 * w0)).astype(jnp.bfloat16)
 
             pieces(step)
-            local, to_right, to_left, to_twin = stores(i)
-
-            @pl.when(z < CHIPS - 1)
-            def _():
-                to_right.start()
-
-            @pl.when(z > 0)
-            def _():
-                to_left.start()
-
-            to_twin.start()
-            for copy in local:
-                copy.start()
-
-    def forwards(i, o, to):
-        which, layer, rows = place(i)
+
+            @pl.when(i >= n - per_layer)
+            def _():
+                def keep(rows):
+                    last_w[d, pl.ds(pl.multiple_of(base.start + rows.start, 8), PIECE)] = wo[s, rows]
+
+                pieces(keep)
+
+            for here, there in spots(i, d):
+
+                @pl.when(here)
+                def _(there=there):
+                    local, to_right, to_left, to_twin = stores(i, there)
+
+                    @pl.when(z < CHIPS - 1)
+                    def _():
+                        to_right.start()
+
+                    @pl.when(z > 0)
+                    def _():
+                        to_left.start()
+
+                    to_twin.start()
+                    if there.memory_space != pltpu.VMEM:
+                        local.start()
+
+    def forwards(i, o, to, there):
         a = lax.rem(i, S_AG)
-        there = new_w.at[which, layer, o * 2 + c, rows]
         return remote(there, there, fwd_s.at[a, o], ag_r.at[a, o], to), remote(there, there, sib_s.at[a, o], sib_r.at[a, o], twin)
 
     def sent(i, o, to, on):
-        ahead, across = forwards(i, o, to)
+        ahead, across = forwards(i, o, to, spots(i, 0)[0][1])
 
         @pl.when(on)
         def _():
@@ -308,14 +327,18 @@
                 def _():
                     sent(i - S_AG, o, to, on)
 
-                ahead, across = forwards(i, o, to)
-                ahead.wait_recv()
-
-                @pl.when(on)
-                def _():
-                    ahead.start()
-
-                across.start()
+                forwards(i, o, to, spots(i, 0)[0][1])[0].wait_recv()
+                for here, there in spots(i, o * 2 + c):
+
+                    @pl.when(here)
+                    def _(there=there):
+                        ahead, across = forwards(i, o, to, there)
+
+                        @pl.when(on)
+                        def _():
+                            ahead.start()
+
+                        across.start()
 
             return 0
 
@@ -327,7 +350,7 @@
 
             @pl.when(inside(i))
             def _():
-                forwards(i, o, right)[1].wait_recv()
+                forwards(i, o, right, spots(i, 0)[0][1])[1].wait_recv()
 
             return 0
 
@@ -394,6 +417,41 @@
     lax.fori_loop(0, S_AG, gather_left, 0)
 
 
+def finish(new_w, last_w, state, *refs):
+    outs, (held, in_sem, out_sem, sem) = refs[:9], refs[9:]
+    straight = [pltpu.make_async_copy(last_w, outs[2].at[outs[2].shape[0] - 1], sem.at[6])]
+    for k in range(6):
+        straight.append(pltpu.make_async_copy(state.at[k // 3, k % 3], outs[3 + k], sem.at[k]))
+    span = held.shape[1]
+    per = new_w.shape[2] // span
+
+    def load(j):
+        k, layer, p = j // SPANS, j % SPANS // per, j % per
+        return pltpu.make_async_copy(new_w.at[k, layer, pl.ds(p * span, span)], held.at[j % S_COPY], in_sem.at[j % S_COPY])
+
+    def store(j):
+        k, layer, p = j // SPANS, j % SPANS // per, j % per
+        return pltpu.make_async_copy(held.at[j % S_COPY], outs[k].at[layer, pl.ds(p * span, span)], out_sem.at[j % S_COPY])
+
+    n = 3 * SPANS - per
+    ahead = S_COPY - 3
+    for j in range(ahead):
+        load(j).start()
+    for copy in straight:
+        copy.start()
+    for j in range(n):
+        load(j).wait()
+        store(j).start()
+        if j + ahead < n:
+            if j + ahead >= S_COPY:
+                store(j + ahead - S_COPY).wait()
+            load(j + ahead).start()
+    for j in range(n - S_COPY, n):
+        store(j).wait()
+    for copy in straight:
+        copy.wait()
+
+
 def solution(mesh):
     bf16, f32 = jnp.bfloat16, jnp.float32
 
@@ -406,15 +464,15 @@
         args += [tiles(w).reshape(layers, 2 * CHIPS, block, 128) for w in weights]
         args += [tiles(x) for x in (*m, *v)]
         dma = pltpu.SemaphoreType.DMA
-        new_w, new_m, new_v = pl.pallas_call(
+        new_w, last_w, state = pl.pallas_call(
             functools.partial(kernel, block // rows, layers),
             out_shape=[
                 jax.ShapeDtypeStruct((3, layers, 2 * CHIPS, block, 128), bf16),
-                jax.ShapeDtypeStruct((3, layers, block, 128), f32),
-                jax.ShapeDtypeStruct((3, layers, block, 128), f32),
+                pltpu.VMEM((2 * CHIPS, block, 128), bf16),
+                pltpu.VMEM((2, 3, layers, block, 128), f32),
             ],
-            in_specs=[pl.BlockSpec(memory_space=pl.ANY)] * 12,
-            out_specs=[pl.BlockSpec(memory_space=pl.ANY)] * 3,
+            in_specs=[pl.BlockSpec(memory_space=pltpu.HBM)] * 12,
+            out_specs=[pl.BlockSpec(memory_space=pltpu.HBM)] + [pl.BlockSpec(memory_space=pltpu.VMEM)] * 2,
             scratch_shapes=[
                 pltpu.VMEM((S_RAW, CHIPS, rows, 128), bf16),
                 pltpu.VMEM((S_RAW, CHIPS, rows, 128), bf16),
@@ -423,11 +481,7 @@
                 pltpu.VMEM((S_OUT, CHIPS, rows, 128), bf16),
                 pltpu.VMEM((S_OUT, CHIPS, rows, 128), bf16),
                 pltpu.VMEM((rows, 128), f32),
-                pltpu.VMEM((S_ADAM, rows, 128), f32),
-                pltpu.VMEM((S_ADAM, rows, 128), f32),
                 pltpu.VMEM((S_ADAM, rows, 128), bf16),
-                pltpu.VMEM((S_ADAM, rows, 128), f32),
-                pltpu.VMEM((S_ADAM, rows, 128), f32),
                 pltpu.VMEM((S_ADAM, rows, 128), bf16),
                 dma((S_RAW,)),
                 dma((S_RAW,)),
@@ -437,18 +491,26 @@
                 dma((S_OUT, CHIPS)),
                 dma((S_IN, CHIPS)),
                 dma((S_ADAM, 3)),
-                dma((S_ADAM, 3)),
+                dma((S_ADAM,)),
                 dma((S_ADAM, 3)),
                 dma((S_AG, CHIPS)),
                 dma((S_AG, CHIPS)),
                 dma((S_AG, CHIPS)),
                 dma((S_AG, CHIPS)),
             ],
-            compiler_params=pltpu.CompilerParams(collective_id=0, has_side_effects=True),
+            compiler_params=pltpu.CompilerParams(collective_id=0, has_side_effects=True, vmem_limit_bytes=ROOM),
         )(*args)
-        outs = [untiles(new_w[k].reshape(layers, -1, 128), *weights[k].shape[1:]) for k in range(3)]
-        for new, old in ((new_m, m), (new_v, v)):
-            outs += [untiles(new[k], *old[k].shape[1:]) for k in range(3)]
+        flat = [jax.ShapeDtypeStruct((layers, 2 * CHIPS * block, 128), bf16)] * 3 + [jax.ShapeDtypeStruct((layers, block, 128), f32)] * 6
+        span = layers * 2 * CHIPS * block // SPANS
+        outs = pl.pallas_call(
+            finish,
+            out_shape=flat,
+            in_specs=[pl.BlockSpec(memory_space=pltpu.HBM)] + [pl.BlockSpec(memory_space=pltpu.VMEM)] * 2,
+            out_specs=[pl.BlockSpec(memory_space=pltpu.HBM)] * 9,
+            scratch_shapes=[pltpu.VMEM((S_COPY, span, 128), bf16), dma((S_COPY,)), dma((S_COPY,)), dma((7,))],
+            compiler_params=pltpu.CompilerParams(vmem_limit_bytes=ROOM),
+        )(new_w.reshape(3, layers, 2 * CHIPS * block, 128), last_w.reshape(2 * CHIPS * block, 128), state)
+        outs = [untiles(o, *old.shape[1:]) for o, old in zip(outs, (*weights, *m, *v), strict=True)]
         return tuple(outs)
 
     all_of, cut = P(None, None, None), P(None, "dp", None)

time: 835 us -> 815 us (0.976)
  local copies, waits for them, and re-layouts: 70.2 us -> 0 us
  Pallas kernels: 763 us -> 813 us
    slice x2 -> x0, local copies, waits for them, and re-layouts: 70.2 us -> none  [the longest x1 46.1 us: step(): new_w[k].reshape(layers, -1, 128)]
    pallas_call x0 -> x1, Pallas kernels: none -> 51.7 us  [step(): pl.pallas_call(finish, out_shape=flat, in_specs=[pl.BlockSpec(memory_spac...]
where the time goes in v2:
time: 815 us; the launch traced here: 814 us
  Pallas kernels  813 us (100%)
    pallas_call x1, Pallas kernels, step(): pl.pallas_call(functools.partial(kernel, block // rows, layers), out_shap...  762 us
    pallas_call x1, Pallas kernels, step(): pl.pallas_call(finish, out_shape=flat, in_specs=[pl.BlockSpec(memory_spac...  51.7 us

profile of v2, /device:TPU:0, one launch (start us, length us, event | category | flops | bytes accessed | tf_op | source)
XLA Modules:
  0.0 814.1 jit_solution(3514891270378375501)
XLA Ops:
  0.6 761.7 %shard_map.187 = (bf16[3,2,8,5600,128]{4,3,2,1,0:T(8,128)(2,1)}, bf16[8,5600,128]{2,1,0:T(8,128)(2,1)S(1)}, f32[2,3,2,5600,128]{4,3,2,1,0:T(8,128)S(1)}) custom-call(bf16[2,4,2,5600,128]{4,3,2,1,0:T(8,128)(2,1)} %bitcast.108, bf16[2,4,2,5600,128]{4,3,2,1,0:T(8,128)(2,1)} %bitcast.109, bf16[2,4,2,5600,128]{4,3,2,1,0:T(8,128)(2,1)} %bitcast.110, ...), custom_call_target="tpu_custom_call" | custom-call | tf_op jit(solution)/shard_map/pallas_call | solution.py:467
  762.4 51.7 %shard_map.188 = (bf16[2,44800,128]{2,1,0:T(8,128)(2,1)}, bf16[2,44800,128]{2,1,0:T(8,128)(2,1)}, bf16[2,44800,128]{2,1,0:T(8,128)(2,1)}, f32[2,5600,128]{2,1,0:...) custom-call(bf16[3,2,44800,128]{3,2,1,0:T(8,128)(2,1)} %bitcast.36.n, ...), custom_call_target="tpu_custom_call" | custom-call | tf_op jit(solution)/shard_map/pallas_call | solution.py:505

commit v3 on v2

--- a/solution.py
+++ b/solution.py
@@ -14,8 +14,11 @@
 HOP2 = 1
 LAG = 2
 S_RAW, S_IN, S_OUT, S_ADAM, S_AG = 10, 6, 3, 3, 16
+LATE = 10
+HELD = 15
 ROOM = 9472 * 1024
-SPANS, S_COPY = 32, 12
+SPAN, S_COPY = 2800, 12
+MOST_COST = 10**11
 PIECE = 32
 
 
@@ -33,12 +36,13 @@
     per_layer, layers, *refs
 ):
     g, w, m, v = (refs[i : i + 3] for i in (0, 3, 6, 9))
-    new_w, last_w, state = refs[12:15]
+    new_w, last_w, late_w, late_twin, state = refs[12:17]
     new_m, new_v = state.at[0], state.at[1]
-    own, sib, rin, lin, rout, lout, total, wi, wo = refs[15:24]
-    own_sem, raw_s, raw_r, rs, rr, ls, lr, ld_sem, st_sem, own_s, fwd_s, ag_r, sib_s, sib_r = refs[24:]
+    own, sib, rin, lin, rout, lout, total, wi, wo = refs[17:26]
+    own_sem, raw_s, raw_r, rs, rr, ls, lr, ld_sem, st_sem, own_s, fwd_s, ag_r, sib_s, sib_r = refs[26:]
     rows_per = TILES * 8
     n = len(g) * layers * per_layer
+    early = n - LATE
     d = lax.axis_index("dp")
     z, c = lax.div(d, 2), lax.rem(d, 2)
     right, left, twin = {"dp": lax.rem(d + 2, 8)}, {"dp": lax.rem(d + 6, 8)}, {"dp": z * 2 + 1 - c}
@@ -54,8 +58,8 @@
 
     def spots(i, owner):
         which, layer, rows = place(i)
-        late = i >= n - per_layer
-        return (jnp.logical_not(late), new_w.at[which, layer, owner, rows]), (late, last_w.at[owner, rows])
+        at = pl.ds(pl.multiple_of((i - (early - HELD)) * rows_per, 8), rows_per)
+        return (i < early - HELD, new_w.at[which, layer, owner, rows]), (i >= early - HELD, last_w.at[owner, at])
 
     def inside(i):
         return (i >= 0) & (i < n)
@@ -215,17 +219,17 @@
         (in_hbm, there), _ = spots(i, d)
         local, to_right, to_left, to_twin = stores(i, there)
 
-        @pl.when(in_hbm)
+        @pl.when(in_hbm | (i >= early))
         def _():
             local.wait()
 
         to_twin.wait_send()
 
-        @pl.when(z < CHIPS - 1)
+        @pl.when((i < early) & (z < CHIPS - 1))
         def _():
             to_right.wait_send()
 
-        @pl.when(z > 0)
+        @pl.when((i < early) & (z > 0))
         def _():
             to_left.wait_send()
 
@@ -276,16 +280,22 @@
 
             pieces(step)
 
-            @pl.when(i >= n - per_layer)
+            @pl.when((i >= early - HELD) & (i < early))
             def _():
                 def keep(rows):
-                    last_w[d, pl.ds(pl.multiple_of(base.start + rows.start, 8), PIECE)] = wo[s, rows]
+                    at = (i - (early - HELD)) * rows_per + rows.start
+                    last_w[d, pl.ds(pl.multiple_of(at, 8), PIECE)] = wo[s, rows]
 
                 pieces(keep)
 
+            @pl.when(i >= early)
+            def _():
+                stores(i, late_w.at[i - early])[0].start()
+                stores(i, late_twin.at[i - early])[3].start()
+
             for here, there in spots(i, d):
 
-                @pl.when(here)
+                @pl.when(here & (i < early))
                 def _(there=there):
                     local, to_right, to_left, to_twin = stores(i, there)
 
@@ -321,7 +331,7 @@
             o = z - 1 - k if rightward else z + 1 + k
             i = t - turn(o) - HOP2 * (k + 1)
 
-            @pl.when(inside(i))
+            @pl.when((i >= 0) & (i < early))
             def _():
                 @pl.when(i >= S_AG)
                 def _():
@@ -348,7 +358,7 @@
         def lane(o, _):
             i = t - turn(o) - HOP2 * jnp.abs(z - o) - 2
 
-            @pl.when(inside(i))
+            @pl.when((i >= 0) & ((i < early) | (o == z) & (i < n)))
             def _():
                 forwards(i, o, right, spots(i, 0)[0][1])[1].wait_recv()
 
@@ -367,7 +377,7 @@
         crossing(t)
         return 0
 
-    lax.fori_loop(0, n + LAG + (HOP + HOP2) * (CHIPS - 1) + 3, step, 0)
+    lax.fori_loop(0, LAG + HOP * (CHIPS - 1) + max(n + 2, early + HOP2 * (CHIPS - 1) + 2) + 1, step, 0)
 
     def raw_left(k, _):
         raw(n - S_RAW + k)[1][0][1].wait_send()
@@ -400,7 +410,7 @@
     lax.fori_loop(0, S_ADAM, stores_left, 0)
 
     def gather_left(k, _):
-        i = n - S_AG + k
+        i = early - S_AG + k
 
         def of_left(o, _):
             sent(i, o, right, z < CHIPS - 1)
@@ -417,27 +427,22 @@
     lax.fori_loop(0, S_AG, gather_left, 0)
 
 
-def finish(new_w, last_w, state, *refs):
-    outs, (held, in_sem, out_sem, sem) = refs[:9], refs[9:]
-    straight = [pltpu.make_async_copy(last_w, outs[2].at[outs[2].shape[0] - 1], sem.at[6])]
-    for k in range(6):
-        straight.append(pltpu.make_async_copy(state.at[k // 3, k % 3], outs[3 + k], sem.at[k]))
-    span = held.shape[1]
-    per = new_w.shape[2] // span
+def write_out(through, straight, held, in_sem, out_sem, sem):
+    n, ahead = len(through), S_COPY - 3
+
+    def slot(j):
+        return held.at[j % S_COPY, pl.ds(0, through[j][0].shape[0])]
 
     def load(j):
-        k, layer, p = j // SPANS, j % SPANS // per, j % per
-        return pltpu.make_async_copy(new_w.at[k, layer, pl.ds(p * span, span)], held.at[j % S_COPY], in_sem.at[j % S_COPY])
+        return pltpu.make_async_copy(through[j][0], slot(j), in_sem.at[j % S_COPY])
 
     def store(j):
-        k, layer, p = j // SPANS, j % SPANS // per, j % per
-        return pltpu.make_async_copy(held.at[j % S_COPY], outs[k].at[layer, pl.ds(p * span, span)], out_sem.at[j % S_COPY])
-
-    n = 3 * SPANS - per
-    ahead = S_COPY - 3
+        return pltpu.make_async_copy(slot(j), through[j][1], out_sem.at[j % S_COPY])
+
+    rest = [pltpu.make_async_copy(*pair, sem.at[k]) for k, pair in enumerate(straight)]
     for j in range(ahead):
         load(j).start()
-    for copy in straight:
+    for copy in rest:
         copy.start()
     for j in range(n):
         load(j).wait()
@@ -448,7 +453,48 @@
             load(j + ahead).start()
     for j in range(n - S_COPY, n):
         store(j).wait()
-    for copy in straight:
+    for copy in rest:
+        copy.wait()
+
+
+def spans(source, target, rows):
+    many = source.shape[0]
+    return [(source.at[pl.ds(p, min(rows, many - p))], target.at[pl.ds(p, min(rows, many - p))]) for p in range(0, many, rows)]
+
+
+def write_most(new_w, state, *refs):
+    outs, (held, *sems) = refs[:9], refs[9:]
+    _, layers, owners, block, _ = new_w.shape
+    through = []
+    for k in range(3):
+        for layer in range(layers):
+            there = pl.ds(0, block - (LATE + HELD) * TILES * 8 if (k, layer) == (2, layers - 1) else block)
+            for owner in range(owners):
+                through += spans(new_w.at[k, layer, owner, there], outs[k].at[layer, owner, there], held.shape[1])
+    write_out(through, [(state.at[k // 3, k % 3], outs[3 + k]) for k in range(6)], held, *sems)
+
+
+def write_held(so_far, last_w, out, sem):
+    del so_far
+    rows = TILES * 8
+    copy = pltpu.make_async_copy(last_w, out.at[out.shape[0] - 1, :, pl.ds(out.shape[2] - (LATE + HELD) * rows, HELD * rows)], sem)
+    copy.start()
+    copy.wait()
+
+
+def write_late(so_far, *refs):
+    del so_far
+    blocks, (out, sem) = refs[: 2 * CHIPS], refs[2 * CHIPS :]
+    d = lax.axis_index("dp")
+    z, c = lax.div(d, 2), lax.rem(d, 2)
+    rows = blocks[0].shape[0]
+    copies = []
+    for k, block in enumerate(blocks):
+        owner = lax.rem(z + CHIPS - k % CHIPS, CHIPS) * 2 + (c if k < CHIPS else 1 - c)
+        copies.append(pltpu.make_async_copy(block, out.at[out.shape[0] - 1, owner, pl.ds(out.shape[2] - rows, rows)], sem.at[k]))
+    for copy in copies:
+        copy.start()
+    for copy in copies:
         copy.wait()
 
 
@@ -464,15 +510,18 @@
         args += [tiles(w).reshape(layers, 2 * CHIPS, block, 128) for w in weights]
         args += [tiles(x) for x in (*m, *v)]
         dma = pltpu.SemaphoreType.DMA
-        new_w, last_w, state = pl.pallas_call(
+        in_hbm, in_vmem = pl.BlockSpec(memory_space=pltpu.HBM), pl.BlockSpec(memory_space=pltpu.VMEM)
+        new_w, last_w, late_w, late_twin, state = pl.pallas_call(
             functools.partial(kernel, block // rows, layers),
             out_shape=[
                 jax.ShapeDtypeStruct((3, layers, 2 * CHIPS, block, 128), bf16),
-                pltpu.VMEM((2 * CHIPS, block, 128), bf16),
+                pltpu.VMEM((2 * CHIPS, HELD * rows, 128), bf16),
+                jax.ShapeDtypeStruct((LATE, rows, 128), bf16),
+                jax.ShapeDtypeStruct((LATE, rows, 128), bf16),
                 pltpu.VMEM((2, 3, layers, block, 128), f32),
             ],
-            in_specs=[pl.BlockSpec(memory_space=pltpu.HBM)] * 12,
-            out_specs=[pl.BlockSpec(memory_space=pltpu.HBM)] + [pl.BlockSpec(memory_space=pltpu.VMEM)] * 2,
+            in_specs=[in_hbm] * 12,
+            out_specs=[in_hbm, in_vmem, in_hbm, in_hbm, in_vmem],
             scratch_shapes=[
                 pltpu.VMEM((S_RAW, CHIPS, rows, 128), bf16),
                 pltpu.VMEM((S_RAW, CHIPS, rows, 128), bf16),
@@ -499,17 +548,43 @@
                 dma((S_AG, CHIPS)),
             ],
             compiler_params=pltpu.CompilerParams(collective_id=0, has_side_effects=True, vmem_limit_bytes=ROOM),
-        )(*args)
-        flat = [jax.ShapeDtypeStruct((layers, 2 * CHIPS * block, 128), bf16)] * 3 + [jax.ShapeDtypeStruct((layers, block, 128), f32)] * 6
-        span = layers * 2 * CHIPS * block // SPANS
-        outs = pl.pallas_call(
-            finish,
-            out_shape=flat,
-            in_specs=[pl.BlockSpec(memory_space=pltpu.HBM)] + [pl.BlockSpec(memory_space=pltpu.VMEM)] * 2,
-            out_specs=[pl.BlockSpec(memory_space=pltpu.HBM)] * 9,
-            scratch_shapes=[pltpu.VMEM((S_COPY, span, 128), bf16), dma((S_COPY,)), dma((S_COPY,)), dma((7,))],
-            compiler_params=pltpu.CompilerParams(vmem_limit_bytes=ROOM),
-        )(new_w.reshape(3, layers, 2 * CHIPS * block, 128), last_w.reshape(2 * CHIPS * block, 128), state)
+        )(*(pltpu.with_memory_space_constraint(x, pltpu.HBM) for x in args))
+        every = range(2 * CHIPS)
+        every = range(2 * CHIPS)
+        late = [late_w.reshape(LATE * rows, 128)]
+        late += [lax.ppermute(late[0], "dp", [(d, (d + 2 * k) % (2 * CHIPS)) for d in every]) for k in range(1, CHIPS)]
+        grant = pltpu.CompilerParams(vmem_limit_bytes=ROOM)
+        most = pl.pallas_call(
+            write_most,
+            out_shape=[jax.ShapeDtypeStruct((layers, 2 * CHIPS, block, 128), bf16)] * 3 + [jax.ShapeDtypeStruct((layers, block, 128), f32)] * 6,
+            in_specs=[in_hbm, in_vmem],
+            out_specs=[in_hbm] * 9,
+            scratch_shapes=[pltpu.VMEM((S_COPY, SPAN, 128), bf16), dma((S_COPY,)), dma((S_COPY,)), dma((6,))],
+            compiler_params=grant,
+            cost_estimate=pl.CostEstimate(flops=MOST_COST, bytes_accessed=150 * 10**6, transcendentals=0),
+        )(new_w, state)
+        twins = [late_twin.reshape(LATE * rows, 128)]
+        twins += [lax.ppermute(x, "dp", [(d, d ^ 1) for d in every]) for x in late[1:]]
+        last = pl.pallas_call(
+            write_held,
+            out_shape=jax.ShapeDtypeStruct(most[2].shape, bf16),
+            in_specs=[in_hbm, in_vmem],
+            out_specs=in_hbm,
+            scratch_shapes=[dma],
+            input_output_aliases={0: 0},
+            compiler_params=grant,
+            cost_estimate=pl.CostEstimate(flops=MOST_COST // 16, bytes_accessed=7 * 10**6, transcendentals=0),
+        )(most[2], last_w)
+        last = pl.pallas_call(
+            write_late,
+            out_shape=jax.ShapeDtypeStruct(last.shape, bf16),
+            in_specs=[in_hbm] + [in_vmem] * (2 * CHIPS),
+            out_specs=in_hbm,
+            scratch_shapes=[dma((2 * CHIPS,))],
+            input_output_aliases={0: 0},
+            compiler_params=grant,
+        )(last, *late, *twins)
+        outs = [*(x.reshape(layers, -1, 128) for x in (most[0], most[1], last)), *most[3:]]
         outs = [untiles(o, *old.shape[1:]) for o, old in zip(outs, (*weights, *m, *v), strict=True)]
         return tuple(outs)
 

time: 815 us -> 800 us (0.982)
  Pallas kernels: 813 us -> 796 us
    pallas_call x1, Pallas kernels: 762 us -> 743 us  [step(): pl.pallas_call(functools.partial(kernel, block // rows, layers), out_shap...]
    pallas_call x1 -> x3, Pallas kernels: 51.7 us -> 53.2 us  [the longest x1 48.1 us: step(): pl.pallas_call(write_most, out_shape=[jax.ShapeDtypeStruct((layers, 2 * C...]
  transfers between devices with their start and end apart: 0 -> 6, of which waited for: 0 -> 2; matrix products, arithmetic and copies ran while one was open for 0% -> 0% of each run, Pallas kernels for 0% -> 6%
where the time goes in v3:
time: 800 us; the launch traced here: 799 us
  Pallas kernels  796 us (100%)
    pallas_call x1, Pallas kernels, step(): pl.pallas_call(functools.partial(kernel, block // rows, layers), out_shap...  743 us
    pallas_call x1, Pallas kernels, step(): pl.pallas_call(write_most, out_shape=[jax.ShapeDtypeStruct((layers, 2 * C...  48.1 us
  transfers between devices with their start and end apart: 6, of which 2 were waited for; matrix products, arithmetic and copies ran while one was open for 0% of the time, Pallas kernels for 6%

profile of v3, /device:TPU:0, one launch (start us, length us, event | category | flops | bytes accessed | tf_op | source)
XLA Modules:
  0.0 799.4 jit_solution(1624049060187204301)
XLA Ops:
  0.6 742.6 %shard_map.187 = (bf16[3,2,8,5600,128]{4,3,2,1,0:T(8,128)(2,1)}, bf16[8,3360,128]{2,1,0:T(8,128)(2,1)S(1)}, bf16[10,224,128]{2,1,0:T(8,128)(2,1)S(1)}, bf16[10,2...) custom-call(bf16[2,4,2,5600,128]{4,3,2,1,0:T(8,128)(2,1)} %bitcast.113, bf16[2,4,2,5600,128]{4,3,2,1,0:T(8,128)(2,1)} %bitcast.114, ...), custom_call_target="tpu_custom_call" | custom-call | tf_op jit(solution)/shard_map/pallas_call | solution.py:514
  743.3 0.9 collective-permute-start.2
  744.2 0.0 collective-permute-start.1
  744.2 1.2 collective-permute-start
  745.4 48.1 %shard_map.188 = (bf16[2,8,5600,128]{3,2,1,0:T(8,128)(2,1)}, bf16[2,8,5600,128]{3,2,1,0:T(8,128)(2,1)}, bf16[2,8,5600,128]{3,2,1,0:T(8,128)(2,1)}, f32[2,5600,12...) custom-call(bf16[3,2,8,5600,128]{4,3,2,1,0:T(8,128)(2,1)} %get-tuple, ...), custom_call_target="tpu_custom_call" | custom-call | flops 99999997952 | bytes 150000000 | tf_op jit(solution)/shard_map/pallas_call | solution.py:557
  793.5 0.0 collective-permute-done.2.refs_3_
  793.5 0.1 collective-permute-start.5
  793.6 0.1 collective-permute-done.1.refs_2_
  793.7 0.4 collective-permute-start.4
  794.1 0.0 collective-permute-done.refs_1_
  794.1 0.1 collective-permute-start.3
  794.2 2.9 shard_map.189.so_far
  797.1 0.0 collective-permute-done.5.refs_7_
  797.1 0.0 collective-permute-done.4.refs_6_
  797.1 0.1 collective-permute-done.3.refs_5_
  797.2 2.2 shard_map.190
Async XLA Ops:
  743.3 50.2 %collective-permute-start.2 = (bf16[2240,128]{1,0:T(8,128)(2,1)S(1)}, bf16[2240,128]{1,0:T(8,128)(2,1)S(1)}, u32[]{:S(2)}, u32[]{:S(2)}) collective-permute-start(bf16[2240,128]{1,0:T(8,128)(2,1)S(1)} %bitcast.107), channel_id=1, source_target_pairs={{0,6},{1,7},{2,0},{3,1},{4,2},{5,3},{6,4},{7,5},{8,14},{9,15},{10,... | collective-permute-start | bytes 1720328 | tf_op jit(solution)/shard_map/ppermute | solution.py:555
  744.2 49.5 %collective-permute-start.1 = (bf16[2240,128]{1,0:T(8,128)(2,1)S(1)}, bf16[2240,128]{1,0:T(8,128)(2,1)S(1)}, u32[]{:S(2)}, u32[]{:S(2)}) collective-permute-start(bf16[2240,128]{1,0:T(8,128)(2,1)S(1)} %bitcast.108), channel_id=1, source_target_pairs={{0,4},{1,5},{2,6},{3,7},{4,0},{5,1},{6,2},{7,3},{8,12},{9,13},{10,... | collective-permute-start | bytes 1720328 | tf_op jit(solution)/shard_map/ppermute | solution.py:555
  744.2 49.9 %collective-permute-start = (bf16[2240,128]{1,0:T(8,128)(2,1)S(1)}, bf16[2240,128]{1,0:T(8,128)(2,1)S(1)}, u32[]{:S(2)}, u32[]{:S(2)}) collective-permute-start(bf16[2240,128]{1,0:T(8,128)(2,1)S(1)} %bitcast.109), channel_id=1, source_target_pairs={{0,2},{1,3},{2,4},{3,5},{4,6},{5,7},{6,0},{7,1},{8,10},{9,11},{10,... | collective-permute-start | bytes 1720328 | tf_op jit(solution)/shard_map/ppermute | solution.py:555
  793.5 3.6 collective-permute-start.5
  793.7 3.4 collective-permute-start.4
  794.1 3.1 collective-permute-start.3

commit v4 on v3

--- a/solution.py
+++ b/solution.py
@@ -12,11 +12,11 @@
 TILES = 28
 HOP = 1
 HOP2 = 1
+RUN = 2
 LAG = 2
-S_RAW, S_IN, S_OUT, S_ADAM, S_AG = 10, 6, 3, 3, 16
-LATE = 10
-HELD = 15
-ROOM = 9472 * 1024
+S_RAW, S_IN, S_OUT, S_ADAM, S_AG = 12, 8, 3, 3, 16
+LATE = 9
+ROOM = 11264 * 1024
 SPAN, S_COPY = 2800, 12
 MOST_COST = 10**11
 PIECE = 32
@@ -43,6 +43,7 @@
     rows_per = TILES * 8
     n = len(g) * layers * per_layer
     early = n - LATE
+    kept = n - layers * per_layer
     d = lax.axis_index("dp")
     z, c = lax.div(d, 2), lax.rem(d, 2)
     right, left, twin = {"dp": lax.rem(d + 2, 8)}, {"dp": lax.rem(d + 6, 8)}, {"dp": z * 2 + 1 - c}
@@ -58,8 +59,10 @@
 
     def spots(i, owner):
         which, layer, rows = place(i)
-        at = pl.ds(pl.multiple_of((i - (early - HELD)) * rows_per, 8), rows_per)
-        return (i < early - HELD, new_w.at[which, layer, owner, rows]), (i >= early - HELD, last_w.at[owner, at])
+        at = pl.ds(pl.multiple_of((i - kept) * rows_per, 8), rows_per)
+        return (i < kept, new_w.at[which, layer, owner, rows]), (i >= kept, last_w.at[owner, at])
+
+    block_sized = new_w.at[0, 0, 0, pl.ds(0, rows_per)]
 
     def inside(i):
         return (i >= 0) & (i < n)
@@ -101,11 +104,18 @@
             for one in g
         ]
 
+    def chunks(step, ahead, body):
+        def upto(x):
+            return jnp.clip(jnp.minimum(2 * x, x + ahead), 0, n)
+
+        def one(i, _):
+            body(i)
+            return 0
+
+        lax.fori_loop(upto(step), upto(step + 1), one, 0)
+
     def fetch(t):
-        i = t
-
-        @pl.when(inside(i))
-        def _():
+        def one(i):
             which, copies = raw(i)
 
             @pl.when(i >= S_RAW)
@@ -119,45 +129,46 @@
                     other.start()
                     mine.start()
 
+        chunks(t, RUN, one)
+
     def arrived(i):
         _, copies = raw(i)
         copies[0][0].wait()
         copies[0][1].wait_recv()
 
+    def passes(i, o, rightward):
+        s, e = lax.rem(i, S_OUT), lax.rem(i, S_IN)
+        if rightward:
+            return remote(rout.at[s, o], rin.at[e, o], rs.at[s, o], rr.at[e, o], right)
+        return remote(lout.at[s, o], lin.at[e, o], ls.at[s, o], lr.at[e, o], left)
+
     def passing(t, rightward):
         if rightward:
-            before, box, out, s_sem, r_sem, to = z, rin, rout, rs, rr, right
-            many, has_in = CHIPS - 1 - z, z > 0
-            first = z <= 1
-            lane_of = lambda k: CHIPS - 1 - k
+            before, box, out = z, rin, rout
+            many, has_in, first = CHIPS - 1 - z, z > 0, z <= 1
         else:
-            before, box, out, s_sem, r_sem, to = CHIPS - 1 - z, lin, lout, ls, lr, left
-            many, has_in = z, z < CHIPS - 1
-            first = z > 1
-            lane_of = lambda k: k
-        i = t - LAG - HOP * before
-
-        @pl.when(inside(i))
+            before, box, out = CHIPS - 1 - z, lin, lout
+            many, has_in, first = z, z < CHIPS - 1, z > 1
+        now = t - LAG - HOP * before
+
+        @pl.when(first)
         def _():
-            raw_slot, in_slot, out_slot = lax.rem(i, S_RAW), lax.rem(i, S_IN), lax.rem(i, S_OUT)
-
-            def copy(o):
-                return remote(out.at[out_slot, o], box.at[in_slot, o], s_sem.at[out_slot, o], r_sem.at[in_slot, o], to)
-
-            @pl.when(first)
-            def _():
-                arrived(i)
-
-            def lane(k, _):
-                o = lane_of(k)
+            chunks(now, RUN, arrived)
+
+        def lane(k, _):
+            o = CHIPS - 1 - k if rightward else k
+
+            def one(i):
+                raw_slot, in_slot, out_slot = lax.rem(i, S_RAW), lax.rem(i, S_IN), lax.rem(i, S_OUT)
+                copy = passes(i, o, rightward)
 
                 @pl.when(i >= S_OUT)
                 def _():
-                    copy(o).wait_send()
+                    copy.wait_send()
 
                 @pl.when(has_in)
                 def _():
-                    copy(o).wait_recv()
+                    copy.wait_recv()
 
                     def add(rows):
                         so_far = f32(own.at[raw_slot, o, rows]) + f32(sib.at[raw_slot, o, rows])
@@ -173,14 +184,12 @@
 
                     pieces(add)
 
-                copy(o).start()
-                return 0
-
-            lax.fori_loop(0, many, lane, 0)
-
-            @pl.when(has_in)
-            def _():
-                copy(z).wait_recv()
+                copy.start()
+
+            chunks(now, jnp.minimum(CHIPS - 2 - k, RUN), one)
+            return 0
+
+        lax.fori_loop(0, many, lane, 0)
 
     def loads(i):
         which, layer, rows = place(i)
@@ -216,10 +225,9 @@
         return local, to_right, to_left, to_twin
 
     def stored(i):
-        (in_hbm, there), _ = spots(i, d)
-        local, to_right, to_left, to_twin = stores(i, there)
-
-        @pl.when(in_hbm | (i >= early))
+        local, to_right, to_left, to_twin = stores(i, block_sized)
+
+        @pl.when((i < kept) | (i >= early))
         def _():
             local.wait()
 
@@ -254,6 +262,8 @@
 
             @pl.when(z > 0)
             def _():
+                passes(i, z, True).wait_recv()
+
                 def add(rows):
                     total[rows] += f32(rin.at[in_slot, z, rows])
 
@@ -261,6 +271,8 @@
 
             @pl.when(z < CHIPS - 1)
             def _():
+                passes(i, z, False).wait_recv()
+
                 def add(rows):
                     total[rows] += f32(lin.at[in_slot, z, rows])
 
@@ -280,10 +292,10 @@
 
             pieces(step)
 
-            @pl.when((i >= early - HELD) & (i < early))
+            @pl.when((i >= kept) & (i < early))
             def _():
                 def keep(rows):
-                    at = (i - (early - HELD)) * rows_per + rows.start
+                    at = (i - kept) * rows_per + rows.start
                     last_w[d, pl.ds(pl.multiple_of(at, 8), PIECE)] = wo[s, rows]
 
                 pieces(keep)
@@ -316,7 +328,7 @@
         return remote(there, there, fwd_s.at[a, o], ag_r.at[a, o], to), remote(there, there, sib_s.at[a, o], sib_r.at[a, o], twin)
 
     def sent(i, o, to, on):
-        ahead, across = forwards(i, o, to, spots(i, 0)[0][1])
+        ahead, across = forwards(i, o, to, block_sized)
 
         @pl.when(on)
         def _():
@@ -337,7 +349,7 @@
                 def _():
                     sent(i - S_AG, o, to, on)
 
-                forwards(i, o, to, spots(i, 0)[0][1])[0].wait_recv()
+                forwards(i, o, to, block_sized)[0].wait_recv()
                 for here, there in spots(i, o * 2 + c):
 
                     @pl.when(here)
@@ -360,7 +372,7 @@
 
             @pl.when((i >= 0) & ((i < early) | (o == z) & (i < n)))
             def _():
-                forwards(i, o, right, spots(i, 0)[0][1])[1].wait_recv()
+                forwards(i, o, right, block_sized)[1].wait_recv()
 
             return 0
 
@@ -386,15 +398,12 @@
     lax.fori_loop(0, S_RAW, raw_left, 0)
 
     def pass_left(k, _):
-        i = n - S_OUT + k
-        s, e = lax.rem(i, S_OUT), lax.rem(i, S_IN)
-
         def to_right(o, _):
-            remote(rout.at[s, o], rin.at[e, o], rs.at[s, o], rr.at[e, o], right).wait_send()
+            passes(n - S_OUT + k, o, True).wait_send()
             return 0
 
         def to_left(o, _):
-            remote(lout.at[s, o], lin.at[e, o], ls.at[s, o], lr.at[e, o], left).wait_send()
+            passes(n - S_OUT + k, o, False).wait_send()
             return 0
 
         lax.fori_loop(z + 1, CHIPS, to_right, 0)
@@ -429,6 +438,7 @@
 
 def write_out(through, straight, held, in_sem, out_sem, sem):
     n, ahead = len(through), S_COPY - 3
+    assert n >= S_COPY
 
     def slot(j):
         return held.at[j % S_COPY, pl.ds(0, through[j][0].shape[0])]
@@ -462,22 +472,25 @@
     return [(source.at[pl.ds(p, min(rows, many - p))], target.at[pl.ds(p, min(rows, many - p))]) for p in range(0, many, rows)]
 
 
-def write_most(new_w, state, *refs):
+def write_most(new_w, last_w, state, *refs):
     outs, (held, *sems) = refs[:9], refs[9:]
-    _, layers, owners, block, _ = new_w.shape
+    layers, owners, block, _ = outs[2].shape
     through = []
-    for k in range(3):
+    for k in range(2):
         for layer in range(layers):
-            there = pl.ds(0, block - (LATE + HELD) * TILES * 8 if (k, layer) == (2, layers - 1) else block)
             for owner in range(owners):
-                through += spans(new_w.at[k, layer, owner, there], outs[k].at[layer, owner, there], held.shape[1])
-    write_out(through, [(state.at[k // 3, k % 3], outs[3 + k]) for k in range(6)], held, *sems)
-
-
-def write_held(so_far, last_w, out, sem):
+                through += spans(new_w.at[k, layer, owner], outs[k].at[layer, owner], held.shape[1])
+    straight = [(last_w.at[:, pl.ds(layer * block, block)], outs[2].at[layer]) for layer in range(layers - 1)]
+    straight += [(state.at[k // 3, k % 3], outs[3 + k]) for k in range(6)]
+    write_out(through, straight, held, *sems)
+
+
+def write_last(so_far, last_w, out, sem):
     del so_far
-    rows = TILES * 8
-    copy = pltpu.make_async_copy(last_w, out.at[out.shape[0] - 1, :, pl.ds(out.shape[2] - (LATE + HELD) * rows, HELD * rows)], sem)
+    layers, _, block, _ = out.shape
+    done = (layers - 1) * block
+    rest = last_w.shape[1] - done
+    copy = pltpu.make_async_copy(last_w.at[:, pl.ds(done, rest)], out.at[layers - 1, :, pl.ds(0, rest)], sem)
     copy.start()
     copy.wait()
 
@@ -490,7 +503,7 @@
     rows = blocks[0].shape[0]
     copies = []
     for k, block in enumerate(blocks):
-        owner = lax.rem(z + CHIPS - k % CHIPS, CHIPS) * 2 + (c if k < CHIPS else 1 - c)
+        owner = lax.rem(z + k, CHIPS) * 2 + (c if k < CHIPS else 1 - c)
         copies.append(pltpu.make_async_copy(block, out.at[out.shape[0] - 1, owner, pl.ds(out.shape[2] - rows, rows)], sem.at[k]))
     for copy in copies:
         copy.start()
@@ -514,8 +527,8 @@
         new_w, last_w, late_w, late_twin, state = pl.pallas_call(
             functools.partial(kernel, block // rows, layers),
             out_shape=[
-                jax.ShapeDtypeStruct((3, layers, 2 * CHIPS, block, 128), bf16),
-                pltpu.VMEM((2 * CHIPS, HELD * rows, 128), bf16),
+                jax.ShapeDtypeStruct((2, layers, 2 * CHIPS, block, 128), bf16),
+                pltpu.VMEM((2 * CHIPS, layers * block - LATE * rows, 128), bf16),
                 jax.ShapeDtypeStruct((LATE, rows, 128), bf16),
                 jax.ShapeDtypeStruct((LATE, rows, 128), bf16),
                 pltpu.VMEM((2, 3, layers, block, 128), f32),
@@ -549,24 +562,25 @@
             ],
             compiler_params=pltpu.CompilerParams(collective_id=0, has_side_effects=True, vmem_limit_bytes=ROOM),
         )(*(pltpu.with_memory_space_constraint(x, pltpu.HBM) for x in args))
+        last_w, state = (pltpu.with_memory_space_constraint(x, pltpu.VMEM) for x in (last_w, state))
         every = range(2 * CHIPS)
         every = range(2 * CHIPS)
         late = [late_w.reshape(LATE * rows, 128)]
-        late += [lax.ppermute(late[0], "dp", [(d, (d + 2 * k) % (2 * CHIPS)) for d in every]) for k in range(1, CHIPS)]
+        late += [lax.ppermute(late[0], "dp", [((d + 2 * k) % (2 * CHIPS), d) for d in every]) for k in range(1, CHIPS)]
         grant = pltpu.CompilerParams(vmem_limit_bytes=ROOM)
         most = pl.pallas_call(
             write_most,
             out_shape=[jax.ShapeDtypeStruct((layers, 2 * CHIPS, block, 128), bf16)] * 3 + [jax.ShapeDtypeStruct((layers, block, 128), f32)] * 6,
-            in_specs=[in_hbm, in_vmem],
+            in_specs=[in_hbm, in_vmem, in_vmem],
             out_specs=[in_hbm] * 9,
-            scratch_shapes=[pltpu.VMEM((S_COPY, SPAN, 128), bf16), dma((S_COPY,)), dma((S_COPY,)), dma((6,))],
+            scratch_shapes=[pltpu.VMEM((S_COPY, SPAN, 128), bf16), dma((S_COPY,)), dma((S_COPY,)), dma((5 + layers,))],
             compiler_params=grant,
             cost_estimate=pl.CostEstimate(flops=MOST_COST, bytes_accessed=150 * 10**6, transcendentals=0),
-        )(new_w, state)
+        )(new_w, last_w, state)
         twins = [late_twin.reshape(LATE * rows, 128)]
         twins += [lax.ppermute(x, "dp", [(d, d ^ 1) for d in every]) for x in late[1:]]
         last = pl.pallas_call(
-            write_held,
+            write_last,
             out_shape=jax.ShapeDtypeStruct(most[2].shape, bf16),
             in_specs=[in_hbm, in_vmem],
             out_specs=in_hbm,

time: 800 us -> 795 us (level)
  transfers between devices with their start and end apart: 6 -> 6, of which waited for: 2 -> 0; matrix products, arithmetic and copies ran while one was open for 0% -> 0% of each run, Pallas kernels for 6% -> 6%
where the time goes in v4:
time: 795 us
  Pallas kernels  790 us (99%)
    pallas_call x1, Pallas kernels, step(): pl.pallas_call(functools.partial(kernel, block // rows, layers), out_shap...  741 us
    pallas_call x1, Pallas kernels, step(): pl.pallas_call(write_most, out_shape=[jax.ShapeDtypeStruct((layers, 2 * C...  44.6 us
  transfers between devices with their start and end apart: 6, of which 0 were waited for; matrix products, arithmetic and copies ran while one was open for 0% of the time, Pallas kernels for 6%

profile of v4, /device:TPU:0, one launch (start us, length us, event | category | flops | bytes accessed | tf_op | source)
XLA Modules:
  0.0 794.8 jit_solution(4058219208973673974)
XLA Ops:
  0.6 740.6 %shard_map.187 = (bf16[2,2,8,5600,128]{4,3,2,1,0:T(8,128)(2,1)}, bf16[8,9184,128]{2,1,0:T(8,128)(2,1)S(1)}, bf16[9,224,128]{2,1,0:T(8,128)(2,1)}, bf16[9,224,128...) custom-call(bf16[2,4,2,5600,128]{4,3,2,1,0:T(8,128)(2,1)} %bitcast.113, bf16[2,4,2,5600,128]{4,3,2,1,0:T(8,128)(2,1)} %bitcast.114, ...), custom_call_target="tpu_custom_call" | custom-call | tf_op jit(solution)/shard_map/pallas_call | solution.py:527
  741.3 0.8 collective-permute-start
  742.1 1.9 collective-permute-start.1
  744.0 0.3 collective-permute-start.2
  744.3 44.6 %shard_map.188 = (bf16[2,8,5600,128]{3,2,1,0:T(8,128)(2,1)}, bf16[2,8,5600,128]{3,2,1,0:T(8,128)(2,1)}, bf16[2,8,5600,128]{3,2,1,0:T(8,128)(2,1)}, f32[2,5600,12...) custom-call(bf16[2,2,8,5600,128]{4,3,2,1,0:T(8,128)(2,1)} %get-tuple, ...), custom_call_target="tpu_custom_call" | custom-call | flops 99999997952 | bytes 150000000 | tf_op jit(solution)/shard_map/pallas_call | solution.py:571
  788.9 0.0 collective-permute-done.refs_1_
  788.9 0.1 collective-permute-start.3
  789.0 0.0 collective-permute-done.1.refs_2_
  789.0 0.5 collective-permute-start.4
  789.5 0.0 collective-permute-done.2.refs_3_
  789.5 0.1 collective-permute-start.5
  789.6 0.0 copy-start
  789.6 0.0 copy-start.1
  789.6 3.1 shard_map.189.so_far
  792.7 0.0 collective-permute-done.3.refs_5_
  792.7 0.0 collective-permute-done.4.refs_6_
  792.7 0.0 collective-permute-done.5.refs_7_
  792.7 0.0 copy-done
  792.7 0.0 copy-done.1
  792.7 2.1 shard_map.190
Async XLA Ops:
  741.3 47.6 %collective-permute-start = (bf16[2016,128]{1,0:T(8,128)(2,1)}, bf16[2016,128]{1,0:T(8,128)(2,1)S(1)}, u32[]{:S(2)}, u32[]{:S(2)}) collective-permute-start(bf16[2016,128]{1,0:T(8,128)(2,1)} %bitcast.107), channel_id=1, source_target_pairs={{2,0},{3,1},{4,2},{5,3},{6,4},{7,5},{0,6},{1,7},{10,8},{11,9},{12,... | collective-permute-start | bytes 1548296 | tf_op jit(solution)/shard_map/ppermute | solution.py:569
  742.1 46.9 %collective-permute-start.1 = (bf16[2016,128]{1,0:T(8,128)(2,1)}, bf16[2016,128]{1,0:T(8,128)(2,1)S(1)}, u32[]{:S(2)}, u32[]{:S(2)}) collective-permute-start(bf16[2016,128]{1,0:T(8,128)(2,1)} %bitcast.108), channel_id=1, source_target_pairs={{4,0},{5,1},{6,2},{7,3},{0,4},{1,5},{2,6},{3,7},{12,8},{13,9},{14,... | collective-permute-start | bytes 1548296 | tf_op jit(solution)/shard_map/ppermute | solution.py:569
  744.0 45.5 %collective-permute-start.2 = (bf16[2016,128]{1,0:T(8,128)(2,1)}, bf16[2016,128]{1,0:T(8,128)(2,1)S(1)}, u32[]{:S(2)}, u32[]{:S(2)}) collective-permute-start(bf16[2016,128]{1,0:T(8,128)(2,1)} %bitcast.109), channel_id=1, source_target_pairs={{6,0},{7,1},{0,2},{1,3},{2,4},{3,5},{4,6},{5,7},{14,8},{15,9},{8,1... | collective-permute-start | bytes 1548296 | tf_op jit(solution)/shard_map/ppermute | solution.py:569
  788.9 3.7 collective-permute-start.3
  789.0 3.7 collective-permute-start.4
  789.5 3.2 collective-permute-start.5
  789.6 3.1 copy-start
  789.6 3.1 copy-start.1

commit v5 on v4

--- a/solution.py
+++ b/solution.py
@@ -15,10 +15,12 @@
 RUN = 2
 LAG = 2
 S_RAW, S_IN, S_OUT, S_ADAM, S_AG = 12, 8, 3, 3, 16
+SENT = 5
 LATE = 9
 ROOM = 11264 * 1024
 SPAN, S_COPY = 2800, 12
 MOST_COST = 10**11
+AWAY = 0, 1, 3, 2
 PIECE = 32
 
 
@@ -117,11 +119,6 @@
     def fetch(t):
         def one(i):
             which, copies = raw(i)
-
-            @pl.when(i >= S_RAW)
-            def _():
-                copies[0][1].wait_send()
-
             for one, (mine, other) in enumerate(copies):
 
                 @pl.when(which == one)
@@ -251,32 +248,34 @@
             for copy in copies[0]:
                 copy.wait()
 
+            raw(i)[1][0][1].wait_send()
+
             @pl.when(i >= S_ADAM)
             def _():
                 stored(i - S_ADAM)
 
-            def begin(rows):
-                total[rows] = f32(own.at[raw_slot, z, rows]) + f32(sib.at[raw_slot, z, rows])
-
-            pieces(begin)
-
             @pl.when(z > 0)
             def _():
                 passes(i, z, True).wait_recv()
 
-                def add(rows):
-                    total[rows] += f32(rin.at[in_slot, z, rows])
-
-                pieces(add)
-
             @pl.when(z < CHIPS - 1)
             def _():
                 passes(i, z, False).wait_recv()
 
-                def add(rows):
-                    total[rows] += f32(lin.at[in_slot, z, rows])
-
-                pieces(add)
+            def add(boxes):
+                def one(rows):
+                    so_far = f32(own.at[raw_slot, z, rows]) + f32(sib.at[raw_slot, z, rows])
+                    for box in boxes:
+                        so_far += f32(box.at[in_slot, z, rows])
+                    total[rows] = so_far
+
+                pieces(one)
+
+            for here, boxes in ((z == 0, [lin]), (z == CHIPS - 1, [rin]), ((z > 0) & (z < CHIPS - 1), [rin, lin])):
+
+                @pl.when(here)
+                def _(boxes=boxes):
+                    add(boxes)
 
             which, layer, base = place(i)
 
@@ -343,12 +342,12 @@
             o = z - 1 - k if rightward else z + 1 + k
             i = t - turn(o) - HOP2 * (k + 1)
 
+            @pl.when((i >= SENT) & (i < early + SENT))
+            def _():
+                sent(i - SENT, o, to, on)
+
             @pl.when((i >= 0) & (i < early))
             def _():
-                @pl.when(i >= S_AG)
-                def _():
-                    sent(i - S_AG, o, to, on)
-
                 forwards(i, o, to, block_sized)[0].wait_recv()
                 for here, there in spots(i, o * 2 + c):
 
@@ -370,7 +369,7 @@
         def lane(o, _):
             i = t - turn(o) - HOP2 * jnp.abs(z - o) - 2
 
-            @pl.when((i >= 0) & ((i < early) | (o == z) & (i < n)))
+            @pl.when((i >= 0) & (i < early))
             def _():
                 forwards(i, o, right, block_sized)[1].wait_recv()
 
@@ -389,13 +388,7 @@
         crossing(t)
         return 0
 
-    lax.fori_loop(0, LAG + HOP * (CHIPS - 1) + max(n + 2, early + HOP2 * (CHIPS - 1) + 2) + 1, step, 0)
-
-    def raw_left(k, _):
-        raw(n - S_RAW + k)[1][0][1].wait_send()
-        return 0
-
-    lax.fori_loop(0, S_RAW, raw_left, 0)
+    lax.fori_loop(0, LAG + HOP * (CHIPS - 1) + max(n, early + HOP2 * (CHIPS - 1) + max(2, SENT)), step, 0)
 
     def pass_left(k, _):
         def to_right(o, _):
@@ -418,22 +411,11 @@
 
     lax.fori_loop(0, S_ADAM, stores_left, 0)
 
-    def gather_left(k, _):
-        i = early - S_AG + k
-
-        def of_left(o, _):
-            sent(i, o, right, z < CHIPS - 1)
-            return 0
-
-        def of_right(o, _):
-            sent(i, o, left, z > 0)
-            return 0
-
-        lax.fori_loop(0, z, of_left, 0)
-        lax.fori_loop(z + 1, CHIPS, of_right, 0)
+    def late_left(k, _):
+        forwards(early + k, z, right, block_sized)[1].wait_recv()
         return 0
 
-    lax.fori_loop(0, S_AG, gather_left, 0)
+    lax.fori_loop(0, LATE, late_left, 0)
 
 
 def write_out(through, straight, held, in_sem, out_sem, sem):
@@ -452,8 +434,6 @@
     rest = [pltpu.make_async_copy(*pair, sem.at[k]) for k, pair in enumerate(straight)]
     for j in range(ahead):
         load(j).start()
-    for copy in rest:
-        copy.start()
     for j in range(n):
         load(j).wait()
         store(j).start()
@@ -461,6 +441,8 @@
             if j + ahead >= S_COPY:
                 store(j + ahead - S_COPY).wait()
             load(j + ahead).start()
+    for copy in rest:
+        copy.start()
     for j in range(n - S_COPY, n):
         store(j).wait()
     for copy in rest:
@@ -503,7 +485,7 @@
     rows = blocks[0].shape[0]
     copies = []
     for k, block in enumerate(blocks):
-        owner = lax.rem(z + k, CHIPS) * 2 + (c if k < CHIPS else 1 - c)
+        owner = lax.rem(z + AWAY[k % CHIPS], CHIPS) * 2 + (c if k < CHIPS else 1 - c)
         copies.append(pltpu.make_async_copy(block, out.at[out.shape[0] - 1, owner, pl.ds(out.shape[2] - rows, rows)], sem.at[k]))
     for copy in copies:
         copy.start()
@@ -566,7 +548,7 @@
         every = range(2 * CHIPS)
         every = range(2 * CHIPS)
         late = [late_w.reshape(LATE * rows, 128)]
-        late += [lax.ppermute(late[0], "dp", [((d + 2 * k) % (2 * CHIPS), d) for d in every]) for k in range(1, CHIPS)]
+        late += [lax.ppermute(late[0], "dp", [((d + 2 * k) % (2 * CHIPS), d) for d in every]) for k in AWAY[1:]]
         grant = pltpu.CompilerParams(vmem_limit_bytes=ROOM)
         most = pl.pallas_call(
             write_most,

time: 795 us -> 793 us (level)
  transfers between devices with their start and end apart: 6 -> 6, of which waited for: 0 -> 1; matrix products, arithmetic and copies ran while one was open for 0% -> 0% of each run, Pallas kernels for 6% -> 6%
where the time goes in v5:
time: 793 us
  Pallas kernels  789 us (99%)
    pallas_call x1, Pallas kernels, step(): pl.pallas_call(functools.partial(kernel, block // rows, layers), out_shap...  739 us
    pallas_call x1, Pallas kernels, step(): pl.pallas_call(write_most, out_shape=[jax.ShapeDtypeStruct((layers, 2 * C...  44 us
  transfers between devices with their start and end apart: 6, of which 1 were waited for; matrix products, arithmetic and copies ran while one was open for 0% of the time, Pallas kernels for 6%

profile of v5, /device:TPU:0, one launch (start us, length us, event | category | flops | bytes accessed | tf_op | source)
XLA Modules:
  0.0 793.0 jit_solution(17658564197982365066)
XLA Ops:
  0.6 739.4 %shard_map.187 = (bf16[2,2,8,5600,128]{4,3,2,1,0:T(8,128)(2,1)}, bf16[8,9184,128]{2,1,0:T(8,128)(2,1)S(1)}, bf16[9,224,128]{2,1,0:T(8,128)(2,1)}, bf16[9,224,128...) custom-call(bf16[2,4,2,5600,128]{4,3,2,1,0:T(8,128)(2,1)} %bitcast.113, bf16[2,4,2,5600,128]{4,3,2,1,0:T(8,128)(2,1)} %bitcast.114, ...), custom_call_target="tpu_custom_call" | custom-call | tf_op jit(solution)/shard_map/pallas_call | solution.py:509
  740.1 0.7 collective-permute-start
  740.8 1.4 collective-permute-start.1
  742.2 0.7 collective-permute-start.2
  742.9 44.0 %shard_map.188 = (bf16[2,8,5600,128]{3,2,1,0:T(8,128)(2,1)}, bf16[2,8,5600,128]{3,2,1,0:T(8,128)(2,1)}, bf16[2,8,5600,128]{3,2,1,0:T(8,128)(2,1)}, f32[2,5600,12...) custom-call(bf16[2,2,8,5600,128]{4,3,2,1,0:T(8,128)(2,1)} %get-tuple, ...), custom_call_target="tpu_custom_call" | custom-call | flops 99999997952 | bytes 150000000 | tf_op jit(solution)/shard_map/pallas_call | solution.py:553
  786.8 0.0 collective-permute-done.refs_1_
  786.9 0.1 collective-permute-start.3
  786.9 0.0 collective-permute-done.1.refs_2_
  786.9 0.5 collective-permute-start.4
  787.4 0.3 collective-permute-done.2.refs_3_
  787.8 0.0 collective-permute-start.5
  787.8 0.0 copy-start
  787.8 0.0 copy-start.1
  787.8 3.1 shard_map.189.so_far
  790.8 0.0 collective-permute-done.3.refs_5_
  790.9 0.0 collective-permute-done.4.refs_6_
  790.9 0.0 collective-permute-done.5.refs_7_
  790.9 0.0 copy-done
  790.9 0.0 copy-done.1
  790.9 2.1 shard_map.190
Async XLA Ops:
  740.1 46.8 %collective-permute-start = (bf16[2016,128]{1,0:T(8,128)(2,1)}, bf16[2016,128]{1,0:T(8,128)(2,1)S(1)}, u32[]{:S(2)}, u32[]{:S(2)}) collective-permute-start(bf16[2016,128]{1,0:T(8,128)(2,1)} %bitcast.107), channel_id=1, source_target_pairs={{2,0},{3,1},{4,2},{5,3},{6,4},{7,5},{0,6},{1,7},{10,8},{11,9},{12,... | collective-permute-start | bytes 1548296 | tf_op jit(solution)/shard_map/ppermute | solution.py:551
  740.8 46.1 %collective-permute-start.1 = (bf16[2016,128]{1,0:T(8,128)(2,1)}, bf16[2016,128]{1,0:T(8,128)(2,1)S(1)}, u32[]{:S(2)}, u32[]{:S(2)}) collective-permute-start(bf16[2016,128]{1,0:T(8,128)(2,1)} %bitcast.108), channel_id=1, source_target_pairs={{6,0},{7,1},{0,2},{1,3},{2,4},{3,5},{4,6},{5,7},{14,8},{15,9},{8,1... | collective-permute-start | bytes 1548296 | tf_op jit(solution)/shard_map/ppermute | solution.py:551
  742.2 45.6 %collective-permute-start.2 = (bf16[2016,128]{1,0:T(8,128)(2,1)}, bf16[2016,128]{1,0:T(8,128)(2,1)S(1)}, u32[]{:S(2)}, u32[]{:S(2)}) collective-permute-start(bf16[2016,128]{1,0:T(8,128)(2,1)} %bitcast.109), channel_id=1, source_target_pairs={{4,0},{5,1},{6,2},{7,3},{0,4},{1,5},{2,6},{3,7},{12,8},{13,9},{14,... | collective-permute-start | bytes 1548296 | tf_op jit(solution)/shard_map/ppermute | solution.py:551
  786.9 4.0 collective-permute-start.3
  786.9 3.9 collective-permute-start.4
  787.8 3.1 collective-permute-start.5
  787.8 3.1 copy-start
  787.8 3.1 copy-start.1

commit v6 on v5

--- a/solution.py
+++ b/solution.py
@@ -9,19 +9,20 @@
 
 MESH = pl.DeviceIdType.MESH
 CHIPS = 4
-TILES = 28
+TILES = 35
 HOP = 1
 HOP2 = 1
 RUN = 2
-LAG = 2
-S_RAW, S_IN, S_OUT, S_ADAM, S_AG = 12, 8, 3, 3, 16
+LAG = 1
+S_RAW, S_IN, S_OUT, S_ADAM, S_AG = 8, 7, 2, 3, 16
 SENT = 5
-LATE = 9
-ROOM = 11264 * 1024
-SPAN, S_COPY = 2800, 12
+MORE = 4
+LATE = 7
+ROOM = 8960 * 1024
+SPAN, S_COPY = 1400, 24
 MOST_COST = 10**11
 AWAY = 0, 1, 3, 2
-PIECE = 32
+PIECE = 40
 
 
 def tiles(x):
@@ -45,7 +46,7 @@
     rows_per = TILES * 8
     n = len(g) * layers * per_layer
     early = n - LATE
-    kept = n - layers * per_layer
+    kept = n - layers * per_layer - MORE
     d = lax.axis_index("dp")
     z, c = lax.div(d, 2), lax.rem(d, 2)
     right, left, twin = {"dp": lax.rem(d + 2, 8)}, {"dp": lax.rem(d + 6, 8)}, {"dp": z * 2 + 1 - c}
@@ -136,7 +137,7 @@
     def passes(i, o, rightward):
         s, e = lax.rem(i, S_OUT), lax.rem(i, S_IN)
         if rightward:
-            return remote(rout.at[s, o], rin.at[e, o], rs.at[s, o], rr.at[e, o], right)
+            return remote(rout.at[s, o - 1], rin.at[e, o - 1], rs.at[s, o], rr.at[e, o], right)
         return remote(lout.at[s, o], lin.at[e, o], ls.at[s, o], lr.at[e, o], left)
 
     def passing(t, rightward):
@@ -154,6 +155,7 @@
 
         def lane(k, _):
             o = CHIPS - 1 - k if rightward else k
+            slot = o - 1 if rightward else o
 
             def one(i):
                 raw_slot, in_slot, out_slot = lax.rem(i, S_RAW), lax.rem(i, S_IN), lax.rem(i, S_OUT)
@@ -169,7 +171,7 @@
 
                     def add(rows):
                         so_far = f32(own.at[raw_slot, o, rows]) + f32(sib.at[raw_slot, o, rows])
-                        out[out_slot, o, rows] = (so_far + f32(box.at[in_slot, o, rows])).astype(jnp.bfloat16)
+                        out[out_slot, slot, rows] = (so_far + f32(box.at[in_slot, slot, rows])).astype(jnp.bfloat16)
 
                     pieces(add)
 
@@ -177,7 +179,7 @@
                 def _():
                     def add(rows):
                         so_far = f32(own.at[raw_slot, o, rows]) + f32(sib.at[raw_slot, o, rows])
-                        out[out_slot, o, rows] = so_far.astype(jnp.bfloat16)
+                        out[out_slot, slot, rows] = so_far.astype(jnp.bfloat16)
 
                     pieces(add)
 
@@ -265,13 +267,13 @@
             def add(boxes):
                 def one(rows):
                     so_far = f32(own.at[raw_slot, z, rows]) + f32(sib.at[raw_slot, z, rows])
-                    for box in boxes:
-                        so_far += f32(box.at[in_slot, z, rows])
+                    for box, lane in boxes:
+                        so_far += f32(box.at[in_slot, lane, rows])
                     total[rows] = so_far
 
                 pieces(one)
 
-            for here, boxes in ((z == 0, [lin]), (z == CHIPS - 1, [rin]), ((z > 0) & (z < CHIPS - 1), [rin, lin])):
+            for here, boxes in ((z == 0, [(lin, z)]), (z == CHIPS - 1, [(rin, z - 1)]), ((z > 0) & (z < CHIPS - 1), [(rin, z - 1), (lin, z)])):
 
                 @pl.when(here)
                 def _(boxes=boxes):
@@ -419,7 +421,7 @@
 
 
 def write_out(through, straight, held, in_sem, out_sem, sem):
-    n, ahead = len(through), S_COPY - 3
+    n, ahead = len(through), S_COPY - 4
     assert n >= S_COPY
 
     def slot(j):
@@ -457,12 +459,15 @@
 def write_most(new_w, last_w, state, *refs):
     outs, (held, *sems) = refs[:9], refs[9:]
     layers, owners, block, _ = outs[2].shape
+    more = MORE * TILES * 8
     through = []
     for k in range(2):
         for layer in range(layers):
+            there = pl.ds(0, block - more if (k, layer) == (1, layers - 1) else block)
             for owner in range(owners):
-                through += spans(new_w.at[k, layer, owner], outs[k].at[layer, owner], held.shape[1])
-    straight = [(last_w.at[:, pl.ds(layer * block, block)], outs[2].at[layer]) for layer in range(layers - 1)]
+                through += spans(new_w.at[k, layer, owner, there], outs[k].at[layer, owner, there], held.shape[1])
+    straight = [(last_w.at[:, pl.ds(0, more)], outs[1].at[layers - 1, :, pl.ds(block - more, more)])]
+    straight += [(last_w.at[:, pl.ds(more + layer * block, block)], outs[2].at[layer]) for layer in range(layers - 1)]
     straight += [(state.at[k // 3, k % 3], outs[3 + k]) for k in range(6)]
     write_out(through, straight, held, *sems)
 
@@ -470,7 +475,7 @@
 def write_last(so_far, last_w, out, sem):
     del so_far
     layers, _, block, _ = out.shape
-    done = (layers - 1) * block
+    done = (layers - 1) * block + MORE * TILES * 8
     rest = last_w.shape[1] - done
     copy = pltpu.make_async_copy(last_w.at[:, pl.ds(done, rest)], out.at[layers - 1, :, pl.ds(0, rest)], sem)
     copy.start()
@@ -510,7 +515,7 @@
             functools.partial(kernel, block // rows, layers),
             out_shape=[
                 jax.ShapeDtypeStruct((2, layers, 2 * CHIPS, block, 128), bf16),
-                pltpu.VMEM((2 * CHIPS, layers * block - LATE * rows, 128), bf16),
+                pltpu.VMEM((2 * CHIPS, layers * block + (MORE - LATE) * rows, 128), bf16),
                 jax.ShapeDtypeStruct((LATE, rows, 128), bf16),
                 jax.ShapeDtypeStruct((LATE, rows, 128), bf16),
                 pltpu.VMEM((2, 3, layers, block, 128), f32),
@@ -520,10 +525,10 @@
             scratch_shapes=[
                 pltpu.VMEM((S_RAW, CHIPS, rows, 128), bf16),
                 pltpu.VMEM((S_RAW, CHIPS, rows, 128), bf16),
-                pltpu.VMEM((S_IN, CHIPS, rows, 128), bf16),
-                pltpu.VMEM((S_IN, CHIPS, rows, 128), bf16),
-                pltpu.VMEM((S_OUT, CHIPS, rows, 128), bf16),
-                pltpu.VMEM((S_OUT, CHIPS, rows, 128), bf16),
+                pltpu.VMEM((S_IN, CHIPS - 1, rows, 128), bf16),
+                pltpu.VMEM((S_IN, CHIPS - 1, rows, 128), bf16),
+                pltpu.VMEM((S_OUT, CHIPS - 1, rows, 128), bf16),
+                pltpu.VMEM((S_OUT, CHIPS - 1, rows, 128), bf16),
                 pltpu.VMEM((rows, 128), f32),
                 pltpu.VMEM((S_ADAM, rows, 128), bf16),
                 pltpu.VMEM((S_ADAM, rows, 128), bf16),
@@ -555,7 +560,7 @@
             out_shape=[jax.ShapeDtypeStruct((layers, 2 * CHIPS, block, 128), bf16)] * 3 + [jax.ShapeDtypeStruct((layers, block, 128), f32)] * 6,
             in_specs=[in_hbm, in_vmem, in_vmem],
             out_specs=[in_hbm] * 9,
-            scratch_shapes=[pltpu.VMEM((S_COPY, SPAN, 128), bf16), dma((S_COPY,)), dma((S_COPY,)), dma((5 + layers,))],
+            scratch_shapes=[pltpu.VMEM((S_COPY, SPAN, 128), bf16), dma((S_COPY,)), dma((S_COPY,)), dma((6 + layers,))],
             compiler_params=grant,
             cost_estimate=pl.CostEstimate(flops=MOST_COST, bytes_accessed=150 * 10**6, transcendentals=0),
         )(new_w, last_w, state)

time: 793 us -> 795 us (level)
  transfers between devices with their start and end apart: 6 -> 6, of which waited for: 1 -> 0; matrix products, arithmetic and copies ran while one was open for 0% -> 0% of each run, Pallas kernels for 6% -> 6%
where the time goes in v6:
time: 795 us; the launch traced here: 792 us
  Pallas kernels  787 us (99%)
    pallas_call x1, Pallas kernels, step(): pl.pallas_call(functools.partial(kernel, block // rows, layers), out_shap...  739 us
    pallas_call x1, Pallas kernels, step(): pl.pallas_call(write_most, out_shape=[jax.ShapeDtypeStruct((layers, 2 * C...  43.3 us
  transfers between devices with their start and end apart: 6, of which 0 were waited for; matrix products, arithmetic and copies ran while one was open for 0% of the time, Pallas kernels for 6%

profile of v6, /device:TPU:0, one launch (start us, length us, event | category | flops | bytes accessed | tf_op | source)
XLA Modules:
  0.0 792.2 jit_solution(9865608817293885140)
XLA Ops:
  0.6 738.8 %shard_map.187 = (bf16[2,2,8,5600,128]{4,3,2,1,0:T(8,128)(2,1)}, bf16[8,10360,128]{2,1,0:T(8,128)(2,1)S(1)}, bf16[7,280,128]{2,1,0:T(8,128)(2,1)}, bf16[7,280,12...) custom-call(bf16[2,4,2,5600,128]{4,3,2,1,0:T(8,128)(2,1)} %bitcast.113, bf16[2,4,2,5600,128]{4,3,2,1,0:T(8,128)(2,1)} %bitcast.114, ...), custom_call_target="tpu_custom_call" | custom-call | tf_op jit(solution)/shard_map/pallas_call | solution.py:514
  739.4 0.7 collective-permute-start
  740.2 1.3 collective-permute-start.1
  741.5 1.5 collective-permute-start.2
  743.0 43.3 %shard_map.188 = (bf16[2,8,5600,128]{3,2,1,0:T(8,128)(2,1)}, bf16[2,8,5600,128]{3,2,1,0:T(8,128)(2,1)}, bf16[2,8,5600,128]{3,2,1,0:T(8,128)(2,1)}, f32[2,5600,12...) custom-call(bf16[2,2,8,5600,128]{4,3,2,1,0:T(8,128)(2,1)} %get-tuple, ...), custom_call_target="tpu_custom_call" | custom-call | flops 99999997952 | bytes 150000000 | tf_op jit(solution)/shard_map/pallas_call | solution.py:558
  786.3 0.0 collective-permute-done.refs_1_
  786.3 0.1 collective-permute-start.3
  786.4 0.0 collective-permute-done.1.refs_2_
  786.4 0.5 collective-permute-start.4
  786.9 0.0 collective-permute-done.2.refs_3_
  786.9 0.1 collective-permute-start.5
  787.0 0.0 copy-start
  787.0 0.0 copy-start.1
  787.0 3.1 shard_map.189.so_far
  790.1 0.0 collective-permute-done.3.refs_5_
  790.1 0.0 collective-permute-done.4.refs_6_
  790.1 0.0 collective-permute-done.5.refs_7_
  790.2 0.0 copy-done
  790.2 0.0 copy-done.1
  790.2 2.0 shard_map.190
Async XLA Ops:
  739.4 46.9 %collective-permute-start = (bf16[1960,128]{1,0:T(8,128)(2,1)}, bf16[1960,128]{1,0:T(8,128)(2,1)S(1)}, u32[]{:S(2)}, u32[]{:S(2)}) collective-permute-start(bf16[1960,128]{1,0:T(8,128)(2,1)} %bitcast.107), channel_id=1, source_target_pairs={{2,0},{3,1},{4,2},{5,3},{6,4},{7,5},{0,6},{1,7},{10,8},{11,9},{12,... | collective-permute-start | bytes 1505288 | tf_op jit(solution)/shard_map/ppermute | solution.py:556
  740.2 46.3 %collective-permute-start.1 = (bf16[1960,128]{1,0:T(8,128)(2,1)}, bf16[1960,128]{1,0:T(8,128)(2,1)S(1)}, u32[]{:S(2)}, u32[]{:S(2)}) collective-permute-start(bf16[1960,128]{1,0:T(8,128)(2,1)} %bitcast.108), channel_id=1, source_target_pairs={{6,0},{7,1},{0,2},{1,3},{2,4},{3,5},{4,6},{5,7},{14,8},{15,9},{8,1... | collective-permute-start | bytes 1505288 | tf_op jit(solution)/shard_map/ppermute | solution.py:556
  741.5 45.4 %collective-permute-start.2 = (bf16[1960,128]{1,0:T(8,128)(2,1)}, bf16[1960,128]{1,0:T(8,128)(2,1)S(1)}, u32[]{:S(2)}, u32[]{:S(2)}) collective-permute-start(bf16[1960,128]{1,0:T(8,128)(2,1)} %bitcast.109), channel_id=1, source_target_pairs={{4,0},{5,1},{6,2},{7,3},{0,4},{1,5},{2,6},{3,7},{12,8},{13,9},{14,... | collective-permute-start | bytes 1505288 | tf_op jit(solution)/shard_map/ppermute | solution.py:556
  786.3 3.8 collective-permute-start.3
  786.4 3.7 collective-permute-start.4
  786.9 3.2 collective-permute-start.5
  787.0 3.1 copy-start
  787.0 3.1 copy-start.1

commit v7 on v6

--- a/solution.py
+++ b/solution.py
@@ -13,12 +13,12 @@
 HOP = 1
 HOP2 = 1
 RUN = 2
-LAG = 1
-S_RAW, S_IN, S_OUT, S_ADAM, S_AG = 8, 7, 2, 3, 16
+LAG = 2
+S_RAW, S_IN, S_OUT, S_ADAM, S_AG = 9, 7, 2, 3, 16
 SENT = 5
-MORE = 4
+MORE = 3
 LATE = 7
-ROOM = 8960 * 1024
+ROOM = 9728 * 1024
 SPAN, S_COPY = 1400, 24
 MOST_COST = 10**11
 AWAY = 0, 1, 3, 2

time: 795 us -> 793 us (level)
  no operation moved by 1% of the time
where the time goes in v7:
time: 793 us; the launch traced here: 792 us
  Pallas kernels  787 us (99%)
    pallas_call x1, Pallas kernels, step(): pl.pallas_call(functools.partial(kernel, block // rows, layers), out_shap...  739 us
    pallas_call x1, Pallas kernels, step(): pl.pallas_call(write_most, out_shape=[jax.ShapeDtypeStruct((layers, 2 * C...  43.4 us
  transfers between devices with their start and end apart: 6, of which 0 were waited for; matrix products, arithmetic and copies ran while one was open for 0% of the time, Pallas kernels for 6%

profile of v7, /device:TPU:0, one launch (start us, length us, event | category | flops | bytes accessed | tf_op | source)
XLA Modules:
  0.0 792.3 jit_solution(737229685032293361)
XLA Ops:
  0.6 738.8 %shard_map.187 = (bf16[2,2,8,5600,128]{4,3,2,1,0:T(8,128)(2,1)}, bf16[8,10080,128]{2,1,0:T(8,128)(2,1)S(1)}, bf16[7,280,128]{2,1,0:T(8,128)(2,1)}, bf16[7,280,12...) custom-call(bf16[2,4,2,5600,128]{4,3,2,1,0:T(8,128)(2,1)} %bitcast.113, bf16[2,4,2,5600,128]{4,3,2,1,0:T(8,128)(2,1)} %bitcast.114, ...), custom_call_target="tpu_custom_call" | custom-call | tf_op jit(solution)/shard_map/pallas_call | solution.py:514
  739.5 0.7 collective-permute-start
  740.2 1.3 collective-permute-start.1
  741.5 1.5 collective-permute-start.2
  743.0 43.4 %shard_map.188 = (bf16[2,8,5600,128]{3,2,1,0:T(8,128)(2,1)}, bf16[2,8,5600,128]{3,2,1,0:T(8,128)(2,1)}, bf16[2,8,5600,128]{3,2,1,0:T(8,128)(2,1)}, f32[2,5600,12...) custom-call(bf16[2,2,8,5600,128]{4,3,2,1,0:T(8,128)(2,1)} %get-tuple, ...), custom_call_target="tpu_custom_call" | custom-call | flops 99999997952 | bytes 150000000 | tf_op jit(solution)/shard_map/pallas_call | solution.py:558
  786.5 0.0 collective-permute-done.refs_1_
  786.5 0.1 collective-permute-start.3
  786.6 0.0 collective-permute-done.1.refs_2_
  786.6 0.5 collective-permute-start.4
  787.1 0.0 collective-permute-done.2.refs_3_
  787.1 0.1 collective-permute-start.5
  787.1 0.0 copy-start
  787.1 0.0 copy-start.1
  787.2 3.1 shard_map.189.so_far
  790.3 0.0 collective-permute-done.3.refs_5_
  790.3 0.0 collective-permute-done.4.refs_6_
  790.3 0.0 collective-permute-done.5.refs_7_
  790.3 0.0 copy-done
  790.3 0.0 copy-done.1
  790.3 2.0 shard_map.190
Async XLA Ops:
  739.5 47.0 %collective-permute-start = (bf16[1960,128]{1,0:T(8,128)(2,1)}, bf16[1960,128]{1,0:T(8,128)(2,1)S(1)}, u32[]{:S(2)}, u32[]{:S(2)}) collective-permute-start(bf16[1960,128]{1,0:T(8,128)(2,1)} %bitcast.107), channel_id=1, source_target_pairs={{2,0},{3,1},{4,2},{5,3},{6,4},{7,5},{0,6},{1,7},{10,8},{11,9},{12,... | collective-permute-start | bytes 1505288 | tf_op jit(solution)/shard_map/ppermute | solution.py:556
  740.2 46.4 %collective-permute-start.1 = (bf16[1960,128]{1,0:T(8,128)(2,1)}, bf16[1960,128]{1,0:T(8,128)(2,1)S(1)}, u32[]{:S(2)}, u32[]{:S(2)}) collective-permute-start(bf16[1960,128]{1,0:T(8,128)(2,1)} %bitcast.108), channel_id=1, source_target_pairs={{6,0},{7,1},{0,2},{1,3},{2,4},{3,5},{4,6},{5,7},{14,8},{15,9},{8,1... | collective-permute-start | bytes 1505288 | tf_op jit(solution)/shard_map/ppermute | solution.py:556
  741.5 45.5 %collective-permute-start.2 = (bf16[1960,128]{1,0:T(8,128)(2,1)}, bf16[1960,128]{1,0:T(8,128)(2,1)S(1)}, u32[]{:S(2)}, u32[]{:S(2)}) collective-permute-start(bf16[1960,128]{1,0:T(8,128)(2,1)} %bitcast.109), channel_id=1, source_target_pairs={{4,0},{5,1},{6,2},{7,3},{0,4},{1,5},{2,6},{3,7},{12,8},{13,9},{14,... | collective-permute-start | bytes 1505288 | tf_op jit(solution)/shard_map/ppermute | solution.py:556
  786.5 3.8 collective-permute-start.3
  786.6 3.7 collective-permute-start.4
  787.1 3.2 collective-permute-start.5
  787.1 3.1 copy-start
  787.1 3.1 copy-start.1
